TPU v7x, 256 devices: a whole 4x4x8 slice. The times are simulated.
256 devices in a mesh: grp: 4 (over x), ty: 4 (over z_lo), tx: 16 (over z_hi, y, core).
Axes of the slice: x: 4, y: 4, z: 8 (z_hi: 2, z_lo: 4; z = z_hi * 4 + z_lo), core: 2. Of those that a mesh axis runs over, the one named last changes fastest.
Arguments:
- tracers: float32 [16, 8, 512, 2048], P(None, 'grp', 'ty', 'tx'), may hold values from -1.5 to 3, as said below
- east_velocity: float32 [8, 512, 2048], P('grp', 'ty', 'tx'), may hold values from -0.6 to 0.6
- north_velocity: float32 [8, 512, 2048], P('grp', 'ty', 'tx'), may hold values from -0.6 to 0.6
- surface: float32 [512, 2048], P('ty', 'tx'), may hold values from -1.5 to 1.5
- depth: float32 [512, 2048], P('ty', 'tx'), may hold values from 1 to 3
- wet_mask: int32 [512, 2048], P('ty', 'tx'), may hold values 0 or 1
- river_cells: int32 [256], P(('ty', 'tx')), may hold values from 0 to 16383
- river_loads: float32 [256, 16], P(('ty', 'tx')), may hold values from 0.2 to 2
- kinetics: float32 [16, 16], replicated, may hold values from -0.3 to 0.24, as said below
Outputs:
- new_tracers: float32 [16, 8, 512, 2048], P(None, 'grp', 'ty', 'tx')
- new_east: float32 [8, 512, 2048], P('grp', 'ty', 'tx')
- new_north: float32 [8, 512, 2048], P('grp', 'ty', 'tx')
- new_surface: float32 [512, 2048], P('ty', 'tx')
Inputs may be any that keep to these rules, and one draw needn't show every extreme that they name: `tracers`: tracer 0 lies in -1.5 to 1.5, tracer 1 in -1 to 1, the others in 0.1 to 3. `kinetics`: diagonal entries lie in -0.3 to -0.05. `river_cells`: entry r is row * 128 + column of a cell in the tile of the device that holds entry r.
All inputs are finite; a program needn't handle non-finite values. No bound on the sum of `wet_mask` on one device may be relied on, other than what follows from the above.
Results may differ from a plain program's by a relative error of at most 0.000096.
Values sent between devices are 32-bit elements; how exact they have to be, the bound alone decides.
A program may use at most 64 MiB of HBM per device.

v0:
```python
import jax
import jax.numpy as jnp
from jax import lax
from jax.sharding import PartitionSpec as P

eta_rate = 0.25
gravity_rate = 0.25
baroclinic_rate = 0.4
viscous_rate = 0.1
friction_rate = 0.3
advect_rate = 0.3
mixing_rate = 0.2
haline_coef = 0.8
thermal_coef = 0.2
warming_rate = 0.46


def extended(cells, sides, width):
    for axis, dim in sides:
        count = lax.axis_size(axis)
        ends = count - 1
        head = lax.slice_in_dim(cells, 0, width, axis=dim)
        tail = lax.slice_in_dim(cells, cells.shape[dim] - width, cells.shape[dim], axis=dim)
        cells = jnp.concatenate(
            [
                lax.ppermute(tail, axis, [(i, (i + 1) % count) for i in range(ends)]),
                cells,
                lax.ppermute(head, axis, [((i + 1) % count, i) for i in range(ends)]),
            ],
            axis=dim,
        )
    return cells


def from_everyone(value, axis):
    count = lax.axis_size(axis)
    return lax.all_to_all(
        jnp.broadcast_to(value[None], (count, *value.shape)), axis, 0, 0, tiled=True
    )


def taken_together(value, axis):
    everything = from_everyone(value, axis)
    return jnp.sum(everything, axis=0)


def together(arrays, axis):
    ends = [0]
    for a in arrays:
        ends.append(ends[-1] + a.size)
    subtotal = taken_together(jnp.concatenate([a.ravel() for a in arrays]), axis)
    return tuple((subtotal[b:e].reshape(a.shape) for a, b, e in zip(arrays, ends, ends[1:])))


def carried_in(value, axis, combine, identity):
    count, here = (lax.axis_size(axis), lax.axis_index(axis))
    everything = lax.all_gather(value, axis)
    start = jnp.broadcast_to(jnp.asarray(identity, value.dtype), value.shape)

    def turn(k, before):
        reached = k < here
        new = combine(before, everything[k])
        return jnp.where(reached, new, before)

    return lax.fori_loop(0, count, turn, start)


def passed_along(block, axis, distance):
    devices = range(lax.axis_size(axis))
    route = [(i - distance, i) for i in devices if i - distance in devices]
    return lax.ppermute(block, axis, route)


def face_terms(depth_pad, wet_pad):
    east_open = wet_pad[:, :-1] * wet_pad[:, 1:]
    north_open = wet_pad[:-1, :] * wet_pad[1:, :]
    east_depth = 0.5 * (depth_pad[:, :-1] + depth_pad[:, 1:]) * east_open
    north_depth = 0.5 * (depth_pad[:-1, :] + depth_pad[1:, :]) * north_open
    return (east_open, north_open, east_depth, north_depth)


def laplace(field_pad):
    inner = field_pad[:, 1:-1, 1:-1]
    return (
        field_pad[:, 2:, 1:-1]
        + field_pad[:, :-2, 1:-1]
        + field_pad[:, 1:-1, 2:]
        + field_pad[:, 1:-1, :-2]
        - 4.0 * inner
    )


def advect(tracer_pad, east_flux, north_flux, depth, levels):
    east_speed = east_flux[:, 1:-1, :]
    east_term = (
        jnp.maximum(east_speed, 0.0) * tracer_pad[..., 1:-1, :-1]
        + jnp.minimum(east_speed, 0.0) * tracer_pad[..., 1:-1, 1:]
    )
    north_speed = north_flux[:, :, 1:-1]
    north_term = (
        jnp.maximum(north_speed, 0.0) * tracer_pad[..., :-1, 1:-1]
        + jnp.minimum(north_speed, 0.0) * tracer_pad[..., 1:, 1:-1]
    )
    divergence = (
        east_term[..., 1:] - east_term[..., :-1] + north_term[..., 1:, :] - north_term[..., :-1, :]
    )
    return tracer_pad[..., 1:-1, 1:-1] - advect_rate * levels * divergence / depth


def vertical_mix(advected, level_above, level_below, has_above, has_below):
    return advected + mixing_rate * (
        has_above * (level_above - advected) + has_below * (level_below - advected)
    )


def add_fields(earlier, later):
    return earlier + later


def shards(
    tracers,
    east_velocity,
    north_velocity,
    surface,
    depth,
    wet_mask,
    river_cells,
    river_loads,
    kinetics,
):
    level_count = east_velocity.shape[0]
    levels = level_count * lax.axis_size("grp")
    first_level = lax.axis_index("grp") * level_count
    level_index = first_level + jnp.arange(level_count, dtype=jnp.int32)
    wet_cells = wet_mask.astype(jnp.float32)
    static_pad = extended(jnp.stack([depth, wet_cells]), (("ty", 1), ("tx", 2)), 1)
    depth_pad = static_pad[0]
    east_open, north_open, east_depth, north_depth = face_terms(depth_pad, static_pad[1])
    flow_rim = extended(
        jnp.concatenate([jnp.stack([east_velocity, north_velocity]), tracers], 0),
        (("ty", 2), ("tx", 3)),
        1,
    )
    tracer_pad = flow_rim[2:]
    east_pad, north_pad, salt_pad, heat_pad = (flow_rim[0], flow_rim[1], flow_rim[2], flow_rim[3])
    east_flux = east_pad[:, :, :-1] * east_depth / levels
    north_flux = north_pad[:, :-1, :] * north_depth / levels
    density = haline_coef * salt_pad - thermal_coef * heat_pad
    running = jnp.cumsum(density, 0)
    column_east, column_north = together((jnp.sum(east_flux, 0), jnp.sum(north_flux, 0)), "grp")
    overlying = carried_in(running[-1], "grp", add_fields, jnp.zeros_like(running[-1]))
    divergence = (
        column_east[1:-1, 1:]
        - column_east[1:-1, :-1]
        + column_north[1:, 1:-1]
        - column_north[:-1, 1:-1]
    )
    new_surface = surface - eta_rate * wet_cells * divergence
    east_next = passed_along(new_surface[:, :1], "tx", -1)
    north_next = passed_along(new_surface[:1, :], "ty", -1)
    surface_east = jnp.concatenate([new_surface[:, 1:], east_next], 1) - new_surface
    surface_north = jnp.concatenate([new_surface[1:, :], north_next], 0) - new_surface
    pressure = baroclinic_rate * depth_pad * (overlying + running - 0.5 * density) / levels
    bottom = (level_index == levels - 1).astype(jnp.float32)[:, None, None]
    new_east = east_open[1:-1, 1:] * (
        east_velocity
        - gravity_rate * surface_east
        - (pressure[:, 1:-1, 2:] - pressure[:, 1:-1, 1:-1])
        + viscous_rate * laplace(east_pad)
        - friction_rate * bottom * east_velocity
    )
    new_north = north_open[1:, 1:-1] * (
        north_velocity
        - gravity_rate * surface_north
        - (pressure[:, 2:, 1:-1] - pressure[:, 1:-1, 1:-1])
        + viscous_rate * laplace(north_pad)
        - friction_rate * bottom * north_velocity
    )
    advected = advect(tracer_pad, east_flux, north_flux, depth, levels)
    level_rim = extended(advected, (("grp", 1),), 1)
    has_above = (level_index > 0).astype(jnp.float32)[:, None, None]
    has_below = (level_index < levels - 1).astype(jnp.float32)[:, None, None]
    blended = vertical_mix(advected, level_rim[:, :-2], level_rim[:, 2:], has_above, has_below)
    updated = tracers + wet_cells * (blended - tracers)
    tracer_count = tracers.shape[0]
    warming = jnp.exp(warming_rate * updated[1])
    reaction = jnp.dot(
        kinetics, updated.reshape(tracer_count, -1), precision=lax.Precision.HIGHEST
    ).reshape(updated.shape)
    river_hits = (river_cells[:, None] == jnp.arange(depth.size, dtype=jnp.int32)[None, :]).astype(
        jnp.float32
    )
    source = jnp.dot(river_loads.T, river_hits, precision=lax.Precision.HIGHEST)
    source = source.reshape((tracer_count, 1) + depth.shape)
    level_top = (level_index == 0).astype(jnp.float32)[:, None, None]
    new_tracers = updated + wet_cells * (warming * reaction + level_top * source)
    return (new_tracers, new_east, new_north, new_surface)


def solution(mesh):
    return jax.shard_map(
        shards,
        mesh=mesh,
        in_specs=(
            P(None, "grp", "ty", "tx"),
            P("grp", "ty", "tx"),
            P("grp", "ty", "tx"),
            P("ty", "tx"),
            P("ty", "tx"),
            P("ty", "tx"),
            P(("ty", "tx")),
            P(("ty", "tx"), None),
            P(),
        ),
        out_specs=(
            P(None, "grp", "ty", "tx"),
            P("grp", "ty", "tx"),
            P("grp", "ty", "tx"),
            P("ty", "tx"),
        ),
        check_vma=False,
    )
```

profile of v0, /device:TPU:27, one launch (start us, length us, event | category | flops | bytes accessed | tf_op | source)
XLA Modules:
  0.0 202.1 jit_solution(14325539190320060579)
XLA Ops:
  0.7 3.3 %copy.153 = f32[16,2,128,128]{3,1,2,0:T(2,128)S(1)} copy(f32[16,2,128,128]{3,2,1,0:T(8,128)} %param.11) | data formatting | bytes 4194304 | tf_op args[0]
  4.2 3.5 %collective-permute-start = (f32[18,2,1,128]{3,1,2,0:T(2,128)S(1)}, f32[18,2,1,128]{3,1,2,0:T(2,128)S(1)}, u32[]{:S(2)}, u32[]{:S(2)}) collective-permute-start(f32[18,2,1,128]{3,1,2,0:T(2,128)S(1)} %get-tuple-element.141), channel_id=1, source_target_pairs={{0,16},{16,32},{32,48},{1,17},{17,33},{33,49},{2,18},{18,34},{34,5... | collective-permute-start | bytes 55304 | tf_op jit(solution)/shard_map/ppermute | solution.py:26
  9.1 4.2 %collective-permute-start.4 = (f32[2,1,128]{2,1,0:T(1,128)S(1)}, f32[2,1,128]{2,1,0:T(1,128)S(1)}, u32[]{:S(2)}, u32[]{:S(2)}) collective-permute-start(f32[2,1,128]{2,1,0:T(1,128)S(1)} %get-tuple-element.158), channel_id=1, source_target_pairs={{0,16},{16,32},{32,48},{1,17},{17,33},{33,49},{2,18},{18,34},{34,5... | collective-permute-start | bytes 3080 | tf_op jit(solution)/shard_map/ppermute | solution.py:26
  18.0 9.8 %collective-permute-start.6 = (f32[2,130,1]{2,1,0:T(8,128)S(1)}, f32[2,130,1]{2,1,0:T(8,128)S(1)}, u32[]{:S(2)}, u32[]{:S(2)}) collective-permute-start(f32[2,130,1]{2,1,0:T(8,128)S(1)} %get-tuple-element.154), channel_id=1, source_target_pairs={{0,1},{1,2},{2,3},{3,4},{4,5},{5,6},{6,7},{7,8},{8,9},{9,10},{10,1... | collective-permute-start | bytes 3128 | tf_op jit(solution)/shard_map/ppermute | solution.py:26
  27.7 1.9 collective-permute-start.7
  30.2 2.4 %copy.176 = f32[2,8,128,128]{3,2,1,0:T(8,128)} copy(f32[2,8,128,128]{3,1,2,0:T(8,128)} %convolution_bitcast_fusion) | data formatting | bytes 2097152
  32.6 7.7 %collective-permute-done.7 = f32[2,130,1]{2,1,0:T(8,128)} collective-permute-done((f32[2,130,1]{2,1,0:T(8,128)S(1)}, f32[2,130,1]{2,1,0:T(8,128)}, u32[]{:S(2)}, u32[]{:S(2)}) %collective-permute-start.7) | collective-permute-done | bytes 1072 | tf_op jit(solution)/shard_map/ppermute | solution.py:28
  44.5 4.8 %fusion.55 = (f32[18,2,130,1]{3,1,2,0:T(2,128)}, f32[18,2,130,1]{3,1,2,0:T(2,128)}) fusion(f32[18,2,130,128]{3,1,2,0:T(2,128)S(1)} %pad_maximum_fusion.10), kind=kLoop, calls=%fused_computation.134 | loop fusion | bytes 74880 | tf_op jit(solution)/shard_map/slice | solution.py:23
  49.3 3.4 %copy.145 = f32[18,2,130,1]{2,1,3,0:T(2,128)S(1)} copy(f32[18,2,130,1]{3,1,2,0:T(2,128)} %get-tuple-element.139) | data formatting | bytes 37440 | tf_op jit(solution)/shard_map/slice | solution.py:23
  52.8 2.0 collective-permute-start.2
  54.7 3.5 %copy.146 = f32[18,2,130,1]{2,1,3,0:T(2,128)S(1)} copy(f32[18,2,130,1]{3,1,2,0:T(2,128)} %get-tuple-element.140) | data formatting | bytes 37440 | tf_op jit(solution)/shard_map/slice | solution.py:22
  58.2 2.4 %collective-permute-start.3 = (f32[18,2,130,1]{2,1,3,0:T(2,128)S(1)}, f32[18,2,130,1]{2,1,3,0:T(2,128)S(1)}, u32[]{:S(2)}, u32[]{:S(2)}) collective-permute-start(f32[18,2,130,1]{2,1,3,0:T(2,128)S(1)} %copy.146), channel_id=1, source_target_pairs={{1,0},{2,1},{3,2},{4,3},{5,4},{6,5},{7,6},{8,7},{9,8},{10,9},{11,1... | collective-permute-start | bytes 56168 | tf_op jit(solution)/shard_map/ppermute | solution.py:28
  63.6 3.0 %copy.147 = f32[18,2,130,1]{3,1,2,0:T(2,128)} copy(f32[18,2,130,1]{2,1,3,0:T(2,128)S(1)} %collective-permute-done.2) | data formatting | bytes 37440 | tf_op jit(solution)/shard_map/ppermute | solution.py:26
  66.6 2.9 %collective-permute-done.3 = f32[18,2,130,1]{2,1,3,0:T(2,128)S(1)} collective-permute-done((f32[18,2,130,1]{2,1,3,0:T(2,128)S(1)}, f32[18,2,130,1]{2,1,3,0:T(2,128)S(1)}, u32[]{:S(2)}, u32[]{:S(2)}) %collective-permute-start.3) | collective-permute-done | bytes 18752 | tf_op jit(solution)/shard_map/ppermute | solution.py:28
  69.5 3.0 %copy.148 = f32[18,2,130,1]{3,1,2,0:T(2,128)} copy(f32[18,2,130,1]{2,1,3,0:T(2,128)S(1)} %collective-permute-done.3) | data formatting | bytes 37440 | tf_op jit(solution)/shard_map/ppermute | solution.py:28
  72.5 2.0 maximum_bitcast_fusion.1
  80.6 4.3 %all-to-all-start = ((f32[4,1,33540]{2,1,0:T(1,128)}), f32[4,1,33540]{2,1,0:T(1,128)}, u32[]{:S(2)}, u32[]{:S(2)}) async-start(f32[4,1,33540]{2,1,0:T(1,128)} %broadcast_in_dim.4), calls=%async_computation | async-start | bytes 1077248 | tf_op jit(solution)/shard_map/all_to_all | solution.py:37
  84.9 2.0 fusion.23
  86.9 28.5 %reduce_window_sum.11 = f32[2,130,130]{2,0,1:T(2,128)} reduce-window(f32[2,130,130]{2,0,1:T(2,128)S(1)} %fusion.23, f32[]{:T(128)} %constant.29.clone.1), window={size=2x1x1 pad=1_0x0_0x0_0}, to_apply=%region_3.4 | reduce-window | flops 33800 | bytes 270404 | tf_op jit(solution)/shard_map/jit(cumsum)/reduce_window_sum | solution.py:149
  116.6 11.3 %all_gather.3 = f32[4,130,130]{2,1,0:T(8,128)} all-gather(f32[1,130,130]{2,1,0:T(8,128)S(1)} %copy.162), channel_id=1, replica_groups=mesh['grp'=4,'ty'=4,'tx'=16] {'grp'}, dimensions={0}, use_global_device_ids=true | all-gather | bytes 338000 | tf_op jit(solution)/shard_map/all_gather | solution.py:57
  130.2 11.6 %fusion.1 = f32[16,2,128,129]{3,1,2,0:T(2,128)S(1)} fusion(f32[18,2,130,1]{3,1,2,0:T(2,128)} %copy.148, f32[18,2,1,128]{3,1,2,0:T(2,128)S(1)} %collective-permute-done.1, f32[18,2,1,128]{3,1,2,0:T(2,128)S(1)} %collective-permute-done, f32[16,2,128,128]{3,1,2,0:T(2,128)S(1)} %copy.153, f32[1,2,128,128]{3,1,2,0:T(2,128)S(1)} %get-tuple-element.164, ...), kind=kLoop, calls=%fused_computation.3 | loop fusion | flops 6868992 | bytes 4811328 | tf_op jit(solution)/shard_map/add | solution.py:96
  141.8 2.6 %fusion.4 = f32[16,2,129,128]{3,1,2,0:T(2,128)S(1)} fusion(f32[18,2,1,128]{3,1,2,0:T(2,128)S(1)} %collective-permute-done.1, f32[16,2,128,128]{3,1,2,0:T(2,128)S(1)} %copy.153, f32[1,2,128,128]{3,1,2,0:T(2,128)S(1)} %get-tuple-element.164, f32[1,2,128,128]{3,1,2,0:T(2,128)S(1)} %get-tuple-element.165, f32[18,2,1,128]{3,1,2,0:T(2,128)S(1)} %collective-permute-done, ...), kind=kLoop, calls=%fused_computation.17 | loop fusion | flops 4755456 | bytes 4773888 | tf_op jit(solution)/shard_map/add | solution.py:101
  144.4 4.0 %divide_subtract_fusion = f32[16,2,128,128]{3,1,2,0:T(2,128)S(1)} fusion(f32[16,2,129,128]{3,1,2,0:T(2,128)S(1)} %fusion.4, f32[16,2,128,129]{3,1,2,0:T(2,128)S(1)} %fusion.1, f32[128,128]{1,0:T(8,128)S(1)} %copy-done.7, f32[16,2,128,128]{3,2,1,0:T(8,128)S(1)} %copy-done.2), kind=kLoop, calls=%fused_computation.24 | loop fusion | flops 3145728 | bytes 12648448 | tf_op jit(solution)/shard_map/sub | solution.py:107
  148.5 4.1 %while.14 = (s32[]{:T(128)}, f32[130,130]{1,0:T(8,128)S(1)}, s32[]{:T(128)}, f32[4,130,130]{2,1,0:T(8,128)}, s32[]{:T(128)}, /*index=5*/s32[]{:T(128)}) while((s32[]{:T(128)}, f32[130,130]{1,0:T(8,128)S(1)}, s32[]{:T(128)}, f32[4,130,130]{2,1,0:T(8,128)}, s32[]{:T(128)}, /*index=5*/s32[]{:T(128)}) %tuple.61), condition=%wide.region_5.6_spmd.clone, body=%wide.region_4.5_spmd.clone.sunk | while | flops 50704 | bytes 202893 | solution.py:65
  152.6 3.6 %fusion.56 = (f32[16,1,128,128]{3,1,2,0:T(1,128)}, f32[16,1,128,128]{3,1,2,0:T(1,128)}) fusion(f32[16,2,128,128]{3,1,2,0:T(2,128)S(1)} %divide_subtract_fusion), kind=kLoop, calls=%fused_computation.135 | loop fusion | bytes 4194304 | tf_op jit(solution)/shard_map/slice | solution.py:23
  158.0 4.5 %collective-permute-start.9 = (f32[16,1,128,128]{3,1,2,0:T(1,128)}, f32[16,1,128,128]{3,1,2,0:T(1,128)}, u32[]{:S(2)}, u32[]{:S(2)}) collective-permute-start(f32[16,1,128,128]{3,1,2,0:T(1,128)} %get-tuple-element.144), channel_id=1, source_target_pairs={{64,0},{128,64},{192,128},{65,1},{129,65},{193,129},{66,2},{130,66... | collective-permute-start | bytes 3145736 | tf_op jit(solution)/shard_map/ppermute | solution.py:28
  165.8 2.9 %collective-permute-start.10 = (f32[128,1]{1,0:T(8,128)S(1)}, f32[128,1]{1,0:T(8,128)S(1)}, u32[]{:S(2)}, u32[]{:S(2)}) collective-permute-start(f32[128,1]{1,0:T(8,128)S(1)} %bitcast.54), channel_id=1, source_target_pairs={{1,0},{2,1},{3,2},{4,3},{5,4},{6,5},{7,6},{8,7},{9,8},{10,9},{11,1... | collective-permute-start | bytes 1544 | tf_op jit(solution)/shard_map/ppermute | solution.py:71
  171.7 5.8 %collective-permute-done.10 = f32[128,1]{1,0:T(8,128)S(1)} collective-permute-done((f32[128,1]{1,0:T(8,128)S(1)}, f32[128,1]{1,0:T(8,128)S(1)}, u32[]{:S(2)}, u32[]{:S(2)}) %collective-permute-start.10) | collective-permute-done | bytes 544 | tf_op jit(solution)/shard_map/ppermute | solution.py:71
  182.7 2.5 %collective-permute-done.9 = f32[16,1,128,128]{3,1,2,0:T(1,128)} collective-permute-done((f32[16,1,128,128]{3,1,2,0:T(1,128)}, f32[16,1,128,128]{3,1,2,0:T(1,128)}, u32[]{:S(2)}, u32[]{:S(2)}) %collective-permute-start.9) | collective-permute-done | bytes 1048608 | tf_op jit(solution)/shard_map/ppermute | solution.py:28
  185.2 7.5 %multiply_add_fusion = f32[16,2,128,128]{3,1,2,0:T(2,128)S(1)} fusion(f32[16,2,128,128]{3,1,2,0:T(2,128)S(1)} %copy-done.5, f32[16,1,128,128]{3,1,2,0:T(1,128)} %collective-permute-done.9, f32[16,1,128,128]{3,1,2,0:T(1,128)} %collective-permute-done.8, f32[2]{0:T(128)S(1)} %get-tuple-element.166, f32[2]{0:T(128)S(1)} %copy-done.16, ...), kind=kLoop, calls=%fused_computation.43 | loop fusion | flops 6291456 | bytes 8454160 | tf_op jit(solution)/shard_map/add | solution.py:184
  193.1 3.1 %fusion.18 = f32[2,8,256,128]{3,1,2,0:T(8,128)S(1)} fusion(f32[16,16]{1,0:T(8,128)S(1)} %copy-done, f32[2,8,256,128]{3,2,1,0:T(8,128)S(1)} %bitcast.48), kind=kOutput, calls=%fused_computation.44 | convolution fusion | flops 100663296 | bytes 4195328 | tf_op jit(solution)/shard_map/dot_general | solution.py:187
  197.4 3.1 %fusion.17 = f32[16,2,128,128]{3,1,2,0:T(2,128)S(1)} fusion(f32[16,2,128,128]{3,1,2,0:T(2,128)S(1)} %multiply_add_fusion, f32[16,2,128,128]{3,2,1,0:T(8,128)S(1)} %bitcast.49, f32[16,128,128]{2,1,0:T(8,128)S(1)} %bitcast.50, f32[2,128,128]{2,0,1:T(2,128)S(1)} %fusion.42, f32[128,128]{1,0:T(8,128)S(1)} %get-tuple-element.162, f32[2]{0:T(128)S(1)} %copy-done.17), kind=kLoop, calls=%fused_computation.42 | loop fusion | flops 2621440 | bytes 7536648 | tf_op jit(solution)/shard_map/add | solution.py:196
  (99 shorter events, 43.9 us)
Async XLA Ops:
  0.6 192.4 %copy-start = (f32[16,16]{1,0:T(8,128)S(1)}, f32[16,16]{1,0:T(8,128)}, u32[]{:S(2)}) copy-start(f32[16,16]{1,0:T(8,128)} %param.19) | copy-start | bytes 3076
  0.6 3.3 %copy-start.10 = (f32[2,128,128]{2,1,0:T(8,128)S(1)}, f32[2,128,128]{2,1,0:T(8,128)}, u32[]{:S(2)}) copy-start(f32[2,128,128]{2,1,0:T(8,128)} %param.12) | copy-start | bytes 393220
  0.7 3.3 %copy-start.9 = (f32[2,128,128]{2,1,0:T(8,128)S(1)}, f32[2,128,128]{2,1,0:T(8,128)}, u32[]{:S(2)}) copy-start(f32[2,128,128]{2,1,0:T(8,128)} %param.13) | copy-start | bytes 393220
  4.0 5.1 %copy-start.11 = (s32[128,128]{1,0:T(8,128)S(1)}, s32[128,128]{1,0:T(8,128)}, u32[]{:S(2)}) copy-start(s32[128,128]{1,0:T(8,128)} %param.16) | copy-start | bytes 196612
  4.0 5.2 %copy-start.7 = (f32[128,128]{1,0:T(8,128)S(1)}, f32[128,128]{1,0:T(8,128)}, u32[]{:S(2)}) copy-start(f32[128,128]{1,0:T(8,128)} %param.15) | copy-start | bytes 196612
  4.0 11.3 %copy-start.14 = (f32[4,16]{1,0:T(4,128)S(1)}, f32[4,16]{1,0:T(4,128)}, u32[]{:S(2)}) copy-start(f32[4,16]{1,0:T(4,128)} %param.18) | copy-start | bytes 772
  4.0 11.2 %copy-start.15 = (s32[4]{0:T(128)S(1)}, s32[4]{0:T(128)}, u32[]{:S(2)}) copy-start(s32[4]{0:T(128)} %param.17) | copy-start | bytes 52
  4.2 38.7 %collective-permute-start = (f32[18,2,1,128]{3,1,2,0:T(2,128)S(1)}, f32[18,2,1,128]{3,1,2,0:T(2,128)S(1)}, u32[]{:S(2)}, u32[]{:S(2)}) collective-permute-start(f32[18,2,1,128]{3,1,2,0:T(2,128)S(1)} %get-tuple-element.141), channel_id=1, source_target_pairs={{0,16},{16,32},{32,48},{1,17},{17,33},{33,49},{2,18},{18,34},{34,5... | collective-permute-start | bytes 55304 | tf_op jit(solution)/shard_map/ppermute | solution.py:26
  7.8 35.1 %collective-permute-start.1 = (f32[18,2,1,128]{3,1,2,0:T(2,128)S(1)}, f32[18,2,1,128]{3,1,2,0:T(2,128)S(1)}, u32[]{:S(2)}, u32[]{:S(2)}) collective-permute-start(f32[18,2,1,128]{3,1,2,0:T(2,128)S(1)} %get-tuple-element.142), channel_id=1, source_target_pairs={{16,0},{32,16},{48,32},{17,1},{33,17},{49,33},{18,2},{34,18},{50,3... | collective-permute-start | bytes 55304 | tf_op jit(solution)/shard_map/ppermute | solution.py:28
  9.1 7.7 %collective-permute-start.4 = (f32[2,1,128]{2,1,0:T(1,128)S(1)}, f32[2,1,128]{2,1,0:T(1,128)S(1)}, u32[]{:S(2)}, u32[]{:S(2)}) collective-permute-start(f32[2,1,128]{2,1,0:T(1,128)S(1)} %get-tuple-element.158), channel_id=1, source_target_pairs={{0,16},{16,32},{32,48},{1,17},{17,33},{33,49},{2,18},{18,34},{34,5... | collective-permute-start | bytes 3080 | tf_op jit(solution)/shard_map/ppermute | solution.py:26
  13.3 4.5 %collective-permute-start.5 = (f32[2,1,128]{2,1,0:T(1,128)S(1)}, f32[2,1,128]{2,1,0:T(1,128)S(1)}, u32[]{:S(2)}, u32[]{:S(2)}) collective-permute-start(f32[2,1,128]{2,1,0:T(1,128)S(1)} %get-tuple-element.159), channel_id=1, source_target_pairs={{16,0},{32,16},{48,32},{17,1},{33,17},{49,33},{18,2},{34,18},{50,3... | collective-permute-start | bytes 3080 | tf_op jit(solution)/shard_map/ppermute | solution.py:28
  18.0 14.7 %collective-permute-start.6 = (f32[2,130,1]{2,1,0:T(8,128)S(1)}, f32[2,130,1]{2,1,0:T(8,128)S(1)}, u32[]{:S(2)}, u32[]{:S(2)}) collective-permute-start(f32[2,130,1]{2,1,0:T(8,128)S(1)} %get-tuple-element.154), channel_id=1, source_target_pairs={{0,1},{1,2},{2,3},{3,4},{4,5},{5,6},{6,7},{7,8},{8,9},{9,10},{10,1... | collective-permute-start | bytes 3128 | tf_op jit(solution)/shard_map/ppermute | solution.py:26
  27.7 12.6 %collective-permute-start.7 = (f32[2,130,1]{2,1,0:T(8,128)S(1)}, f32[2,130,1]{2,1,0:T(8,128)}, u32[]{:S(2)}, u32[]{:S(2)}) collective-permute-start(f32[2,130,1]{2,1,0:T(8,128)S(1)} %get-tuple-element.155), channel_id=1, source_target_pairs={{1,0},{2,1},{3,2},{4,3},{5,4},{6,5},{7,6},{8,7},{9,8},{10,9},{11,1... | collective-permute-start | bytes 3128 | tf_op jit(solution)/shard_map/ppermute | solution.py:28
  52.8 10.8 %collective-permute-start.2 = (f32[18,2,130,1]{2,1,3,0:T(2,128)S(1)}, f32[18,2,130,1]{2,1,3,0:T(2,128)S(1)}, u32[]{:S(2)}, u32[]{:S(2)}) collective-permute-start(f32[18,2,130,1]{2,1,3,0:T(2,128)S(1)} %copy.145), channel_id=1, source_target_pairs={{0,1},{1,2},{2,3},{3,4},{4,5},{5,6},{6,7},{7,8},{8,9},{9,10},{10,1... | collective-permute-start | bytes 56168 | tf_op jit(solution)/shard_map/ppermute | solution.py:26
  58.2 11.3 %collective-permute-start.3 = (f32[18,2,130,1]{2,1,3,0:T(2,128)S(1)}, f32[18,2,130,1]{2,1,3,0:T(2,128)S(1)}, u32[]{:S(2)}, u32[]{:S(2)}) collective-permute-start(f32[18,2,130,1]{2,1,3,0:T(2,128)S(1)} %copy.146), channel_id=1, source_target_pairs={{1,0},{2,1},{3,2},{4,3},{5,4},{6,5},{7,6},{8,7},{9,8},{10,9},{11,1... | collective-permute-start | bytes 56168 | tf_op jit(solution)/shard_map/ppermute | solution.py:28
  80.6 82.0 %all-to-all-start = ((f32[4,1,33540]{2,1,0:T(1,128)}), f32[4,1,33540]{2,1,0:T(1,128)}, u32[]{:S(2)}, u32[]{:S(2)}) async-start(f32[4,1,33540]{2,1,0:T(1,128)} %broadcast_in_dim.4), calls=%async_computation | async-start | bytes 1077248 | tf_op jit(solution)/shard_map/all_to_all | solution.py:37
  115.4 14.8 %copy-start.1 = (f32[18,2,130,1]{3,1,2,0:T(2,128)S(1)}, f32[18,2,130,1]{3,1,2,0:T(2,128)}, u32[]{:S(2)}) copy-start(f32[18,2,130,1]{3,1,2,0:T(2,128)} %copy.147) | copy-start | bytes 56164
  141.8 2.6 %copy-start.2 = (f32[16,2,128,128]{3,2,1,0:T(8,128)S(1)}, f32[16,2,128,128]{3,2,1,0:T(8,128)}, u32[]{:S(2)}) copy-start(f32[16,2,128,128]{3,2,1,0:T(8,128)} %param.11) | copy-start | bytes 6291460
  148.5 7.7 %copy-start.4 = (f32[16,2,128,128]{3,1,2,0:T(2,128)}, f32[16,2,128,128]{3,1,2,0:T(2,128)S(1)}, u32[]{:S(2)}) copy-start(f32[16,2,128,128]{3,1,2,0:T(2,128)S(1)} %divide_subtract_fusion) | copy-start | bytes 6291460
  152.6 12.3 %copy-start.12 = (s32[128,128]{1,0:T(8,128)S(1)}, s32[128,128]{1,0:T(8,128)}, u32[]{:S(2)}) copy-start(s32[128,128]{1,0:T(8,128)} %param.16) | copy-start | bytes 196612
  156.1 26.5 %collective-permute-start.8 = (f32[16,1,128,128]{3,1,2,0:T(1,128)}, f32[16,1,128,128]{3,1,2,0:T(1,128)}, u32[]{:S(2)}, u32[]{:S(2)}) collective-permute-start(f32[16,1,128,128]{3,1,2,0:T(1,128)} %get-tuple-element.143), channel_id=1, source_target_pairs={{0,64},{64,128},{128,192},{1,65},{65,129},{129,193},{2,66},{66,130... | collective-permute-start | bytes 3145736 | tf_op jit(solution)/shard_map/ppermute | solution.py:26
  158.0 27.1 %collective-permute-start.9 = (f32[16,1,128,128]{3,1,2,0:T(1,128)}, f32[16,1,128,128]{3,1,2,0:T(1,128)}, u32[]{:S(2)}, u32[]{:S(2)}) collective-permute-start(f32[16,1,128,128]{3,1,2,0:T(1,128)} %get-tuple-element.144), channel_id=1, source_target_pairs={{64,0},{128,64},{192,128},{65,1},{129,65},{193,129},{66,2},{130,66... | collective-permute-start | bytes 3145736 | tf_op jit(solution)/shard_map/ppermute | solution.py:28
  164.3 15.8 %copy-start.13 = (f32[128,128]{1,0:T(8,128)S(1)}, f32[128,128]{1,0:T(8,128)}, u32[]{:S(2)}) copy-start(f32[128,128]{1,0:T(8,128)} %slice.327) | copy-start | bytes 196612
  165.8 16.0 %copy-start.8 = (f32[128,128]{1,0:T(8,128)}, f32[128,128]{1,0:T(8,128)S(1)}, u32[]{:S(2)}) copy-start(f32[128,128]{1,0:T(8,128)S(1)} %fusion.47) | copy-start | bytes 196612
  165.8 11.6 %collective-permute-start.10 = (f32[128,1]{1,0:T(8,128)S(1)}, f32[128,1]{1,0:T(8,128)S(1)}, u32[]{:S(2)}, u32[]{:S(2)}) collective-permute-start(f32[128,1]{1,0:T(8,128)S(1)} %bitcast.54), channel_id=1, source_target_pairs={{1,0},{2,1},{3,2},{4,3},{5,4},{6,5},{7,6},{8,7},{9,8},{10,9},{11,1... | collective-permute-start | bytes 1544 | tf_op jit(solution)/shard_map/ppermute | solution.py:71
  168.7 8.8 %collective-permute-start.11 = (f32[1,128]{1,0:T(1,128)S(1)}, f32[1,128]{1,0:T(1,128)S(1)}, u32[]{:S(2)}, u32[]{:S(2)}) collective-permute-start(f32[1,128]{1,0:T(1,128)S(1)} %slice.346), channel_id=1, source_target_pairs={{16,0},{32,16},{48,32},{17,1},{33,17},{49,33},{18,2},{34,18},{50,3... | collective-permute-start | bytes 1544 | tf_op jit(solution)/shard_map/ppermute | solution.py:71
  170.0 15.2 %copy-start.5 = (f32[16,2,128,128]{3,1,2,0:T(2,128)S(1)}, f32[16,2,128,128]{3,1,2,0:T(2,128)}, u32[]{:S(2)}) copy-start(f32[16,2,128,128]{3,1,2,0:T(2,128)} %copy-done.4) | copy-start | bytes 6291460
  171.5 13.6 %copy-start.3 = (f32[16,2,128,128]{3,2,1,0:T(8,128)S(1)}, f32[16,2,128,128]{3,2,1,0:T(8,128)}, u32[]{:S(2)}) copy-start(f32[16,2,128,128]{3,2,1,0:T(8,128)} %param.11) | copy-start | bytes 6291460
  171.6 13.6 %copy-start.16 = (f32[2]{0:T(128)S(1)}, f32[2]{0:T(128)}, u32[]{:S(2)}) copy-start(f32[2]{0:T(128)} %get-tuple-element.167) | copy-start | bytes 28
  196.2 1.2 copy-start.6
  196.2 1.2 copy-start.17
where the time goes:
time: 206 us; the launch traced here: 202 us
  other arithmetic  85 us (41%)
  starting transfers between devices  41.3 us (20%)
  local copies, waits for them, and re-layouts  38.4 us (19%)
  waiting for transfers between devices  20.1 us (10%)
  blocking collectives  11.3 us (5%)
  matrix products  4.7 us (2%)
    another operation x1, other arithmetic, shards(): running = jnp.cumsum(density, 0)  28.5 us
    ppermute x5, starting transfers between devices, extended(): lax.ppermute(tail, axis, [(i, (i + 1) % count) for i in range(ends)])  21.4 us
    ppermute x5, waiting for transfers between devices, extended(): lax.ppermute(head, axis, [((i + 1) % count, i) for i in range(ends)])  14.1 us
    slice x4, local copies, waits for them, and re-layouts, extended(): lax.slice_in_dim(cells, cells.shape[dim] - width, cells.shape[dim], axis=...  11.9 us
    add x1, other arithmetic, advect(): jnp.maximum(east_speed, 0.0) * tracer_pad[..., 1:-1, :-1]  11.6 us
    ppermute x5, starting transfers between devices, extended(): lax.ppermute(head, axis, [((i + 1) % count, i) for i in range(ends)])  11.4 us
    all_gather x1, blocking collectives, carried_in(): everything = lax.all_gather(value, axis)  11.3 us
    unnamed x42, local copies, waits for them, and re-layouts  9.91 us
  transfers between devices with their start and end apart: 13, of which 6 were waited for; matrix products, arithmetic and copies ran while one was open for 43% of the time, Pallas kernels for 0%

commit v1 on v0

v1 whole, which is shorter than its diff:
```python
import functools

import jax
import jax.numpy as jnp
from jax import lax
from jax.experimental import pallas as pl
from jax.experimental.pallas import tpu as pltpu
from jax.sharding import PartitionSpec as P

f32 = jnp.float32
MESH = pl.DeviceIdType.MESH

eta_rate = 0.25
gravity_rate = 0.25
baroclinic_rate = 0.4
viscous_rate = 0.1
friction_rate = 0.3
advect_rate = 0.3
mixing_rate = 0.2
haline_coef = 0.8
thermal_coef = 0.2
warming_rate = 0.46

PAD = 8
BULK_FIRST = 4
BULK_SECOND = 6
BULK_THIRD = 10


def step_kernel(
    levels,
    tr_hbm, u_hbm, v_hbm, sf_hbm, dp_hbm, wm_hbm, rc_hbm, rl_hbm, kin_hbm,
    out_tr, out_u, out_v, out_s,
    trp, up, vp, sfb, dpp, wmb, wp, kb,
    fb, gp, sb, spb, srecv, db, dpb, drecv,
    ns_send, ns_recv, q, ew_recv, mb,
    xb, xt, xr, yb, bx, adv, ga, gb,
    nsp, pp, c2, c2t, e2, t2, r2, n2,
    rc, rl, kin, load_sem, halo_ss, halo_rs, red_ss, red_rs, x_ss, x_rs, p2_ss, p2_rs, bulk_ss, bulk_rs,
):
    g, gy, gt = lax.axis_index("grp"), lax.axis_index("ty"), lax.axis_index("tx")
    n_grp, n_ty, n_tx = lax.axis_size("grp"), lax.axis_size("ty"), lax.axis_size("tx")
    nt = tr_hbm.shape[0]
    rows, lanes = sfb.shape
    blocks = rows // 8
    n_uv = 2 * nt
    f_d, f_w = n_uv + 4, n_uv + 5

    up_there, down_there = g > 0, g < n_grp - 1
    first = g + 1 - 2 * lax.rem(g, 2)
    second = n_grp - 1 - g

    lane = lax.broadcasted_iota(jnp.int32, (8, lanes), 1)
    sub = lax.broadcasted_iota(jnp.int32, (8, lanes), 0)
    pair = lane // 2
    even = lax.rem(lane, 2) == 0
    at_east, at_west = lane == lanes - 1, lane == 0
    at_edge = jnp.logical_or(at_east, at_west)

    def roll(x, shift):
        shift = shift % lanes
        return x if shift == 0 else pltpu.roll(x, shift, 1)

    def unpacked(tile, field):
        return roll(tile, lanes - 1 - 2 * field)

    def blk(r):
        return pl.ds(pl.multiple_of(r * 8, 8), 8)

    def mid(r):
        return pl.ds(pl.multiple_of(r * 8 + PAD, 8), 8)

    def south(r):
        return pl.ds(r * 8 + (PAD - 1), 8)

    def north(r):
        return pl.ds(r * 8 + (PAD + 1), 8)

    inner = pl.ds(PAD, rows)
    loads = [
        pltpu.make_async_copy(u_hbm, up.at[:, inner, :], load_sem.at[0]),
        pltpu.make_async_copy(v_hbm, vp.at[:, inner, :], load_sem.at[1]),
        pltpu.make_async_copy(dp_hbm, dpp.at[inner, :], load_sem.at[2]),
        pltpu.make_async_copy(wm_hbm, wmb, load_sem.at[3]),
        pltpu.make_async_copy(tr_hbm, trp.at[:, :, inner, :], load_sem.at[4]),
        pltpu.make_async_copy(sf_hbm, sfb, load_sem.at[5]),
        pltpu.make_async_copy(kin_hbm, kin, load_sem.at[6]),
        pltpu.make_async_copy(rc_hbm, rc, load_sem.at[7]),
        pltpu.make_async_copy(rl_hbm, rl, load_sem.at[8]),
    ]
    for load in loads:
        load.start()

    neighbours = [
        (None, {"grp": first}),
        (None, {"grp": second}),
        (gy > 0, {"ty": gy - 1}),
        (gy < n_ty - 1, {"ty": gy + 1}),
        (gt > 0, {"tx": gt - 1}),
        (gt < n_tx - 1, {"tx": gt + 1}),
    ]
    barrier = pltpu.get_barrier_semaphore()
    for there, device in neighbours:
        if there is None:
            pl.semaphore_signal(barrier, inc=1, device_id=device, device_id_type=MESH)
        else:

            @pl.when(there)
            def _(device=device):
                pl.semaphore_signal(barrier, inc=1, device_id=device, device_id_type=MESH)

    def remote(src, dst, ss, rs, device):
        return pltpu.make_async_remote_copy(
            src_ref=src, dst_ref=dst, send_sem=ss, recv_sem=rs, device_id=device, device_id_type=MESH
        )

    to_north = remote(ns_send.at[0], ns_recv.at[0], halo_ss.at[0], halo_rs.at[0], {"ty": gy + 1})
    to_south = remote(ns_send.at[1], ns_recv.at[1], halo_ss.at[1], halo_rs.at[1], {"ty": gy - 1})
    to_east = remote(q, ew_recv.at[0], halo_ss.at[2], halo_rs.at[2], {"tx": gt + 1})
    to_west = remote(q, ew_recv.at[1], halo_ss.at[3], halo_rs.at[3], {"tx": gt - 1})
    halo_sends = [
        (gy < n_ty - 1, to_north),
        (gy > 0, to_south),
        (gt < n_tx - 1, to_east),
        (gt > 0, to_west),
    ]
    halo_recvs = [
        (gy > 0, to_north),
        (gy < n_ty - 1, to_south),
        (gt > 0, to_east),
        (gt < n_tx - 1, to_west),
    ]
    s_first = remote(sb, srecv.at[0], red_ss.at[0], red_rs.at[0], {"grp": first})
    s_second = remote(spb, srecv.at[1], red_ss.at[1], red_rs.at[1], {"grp": second})
    d_first = remote(db, drecv.at[0], red_ss.at[2], red_rs.at[2], {"grp": first})
    d_second = remote(dpb, drecv.at[1], red_ss.at[3], red_rs.at[3], {"grp": second})
    low, high = pl.ds(0, 2 * nt), pl.ds(2 * nt, 2 * nt)
    x_up = remote(xt.at[low, :], xr.at[high, :], x_ss.at[0], x_rs.at[0], {"grp": g - 1})
    x_down = remote(xt.at[high, :], xr.at[low, :], x_ss.at[1], x_rs.at[1], {"grp": g + 1})
    p2_west = remote(
        c2t.at[pl.ds(0, 8), :], e2.at[pl.ds(0, 8), :], p2_ss.at[0], p2_rs.at[0], {"tx": gt - 1}
    )
    p2_south = remote(r2, n2, p2_ss.at[1], p2_rs.at[1], {"ty": gy - 1})

    def bulk_up(r):
        return remote(adv.at[0, r], gb.at[r], bulk_ss.at[0, r], bulk_rs.at[0, r], {"grp": g - 1})

    def bulk_down(r):
        return remote(adv.at[1, r], ga.at[r], bulk_ss.at[1, r], bulk_rs.at[1, r], {"grp": g + 1})

    def send_bulk(r):
        @pl.when(up_there)
        def _():
            bulk_up(r).start()

        @pl.when(down_there)
        def _():
            bulk_down(r).start()

    def loop(start, stop, body):
        lax.fori_loop(start, stop, lambda i, c: (body(i), c)[1], 0)

    zero = jnp.zeros((8, lanes), f32)

    def clear(ref):
        def one(i):
            ref[blk(i), :] = zero

        loop(0, ref.shape[0] // 8, one)

    def clear_ghost(ref):
        def one(i):
            for n in range(nt):
                ref[i, n] = zero

        loop(0, blocks, one)

    @pl.when(jnp.logical_not(up_there))
    def _():
        clear_ghost(ga)
        clear(xr.at[low, :])

    @pl.when(jnp.logical_not(down_there))
    def _():
        clear_ghost(gb)
        clear(xr.at[high, :])

    clear(xr.at[pl.ds(4 * nt, lanes - 4 * nt), :])
    clear(e2.at[pl.ds(8, lanes - 8), :])

    for slot, (there, _) in enumerate(halo_recvs):

        @pl.when(jnp.logical_not(there))
        def _(slot=slot):
            clear(ns_recv.at[slot] if slot < 2 else ew_recv.at[slot - 2])

    @pl.when(gt == n_tx - 1)
    def _():
        e2[pl.ds(0, 8), :] = zero

    @pl.when(gy == n_ty - 1)
    def _():
        n2[...] = zero

    for load in loads[:4]:
        load.wait()
    for edge in (0, PAD + rows):
        dpp[pl.ds(edge, 8), :] = zero
        wp[pl.ds(edge, 8), :] = zero

    def wetness(r):
        wp[mid(r), :] = wmb[blk(r), :].astype(f32)

    loop(0, blocks, wetness)

    def north_face(r):
        d, w = dpp[mid(r), :], wp[mid(r), :]
        depth_n = (0.5 / levels) * (d + dpp[north(r), :]) * (w * wp[north(r), :])
        for l in range(2):
            gp[l, mid(r), :] = vp[l, mid(r), :] * depth_n

    def faces(r):
        d, w = dpp[mid(r), :], wp[mid(r), :]
        depth_e = (0.5 / levels) * (d + roll(d, -1)) * (w * roll(w, -1))
        depth_e = jnp.where(at_east, 0.0, depth_e)
        for l in range(2):
            fb[l, blk(r), :] = up[l, mid(r), :] * depth_e
        north_face(r)

    loop(0, blocks, faces)
    loads[4].wait()

    def edges(r):
        sb[blk(r), :] = haline_coef * (trp[0, 0, mid(r), :] + trp[0, 1, mid(r), :]) - thermal_coef * (
            trp[1, 0, mid(r), :] + trp[1, 1, mid(r), :]
        )
        packed = zero
        fields = [trp[n, l, mid(r), :] for l in range(2) for n in range(nt)]
        fields += [up[0, mid(r), :], up[1, mid(r), :], vp[0, mid(r), :], vp[1, mid(r), :]]
        fields += [dpp[mid(r), :], wp[mid(r), :]]
        for f, field in enumerate(fields):
            packed = jnp.where(pair == f, roll(field, 2 * f + 1), packed)
        q[blk(r), :] = packed

    loop(0, blocks, edges)

    padded = [trp.at[n, l] for l in range(2) for n in range(nt)]
    padded += [up.at[0], up.at[1], vp.at[0], vp.at[1], dpp, wp]
    for f, ref in enumerate(padded):
        ns_send[0, pl.ds(f, 1), :] = ref[pl.ds(PAD + rows - 1, 1), :]
        ns_send[1, pl.ds(f, 1), :] = ref[pl.ds(PAD, 1), :]
    for f in range(len(padded), ns_send.shape[1]):
        for slot in range(2):
            ns_send[slot, pl.ds(f, 1), :] = jnp.zeros((1, lanes), f32)

    peers = sum(1 if there is None else there.astype(jnp.int32) for there, _ in neighbours)
    pl.semaphore_wait(barrier, peers)

    s_first.start()
    for there, copy in reversed(halo_sends):

        @pl.when(there)
        def _(copy=copy):
            copy.start()

    def advect(r):
        d = dpp[mid(r), :]
        scale = (advect_rate * levels) / d
        for l in range(2):
            fe, gn, gs = fb[l, blk(r), :], gp[l, mid(r), :], gp[l, south(r), :]
            fw = roll(fe, 1)
            out = (jnp.maximum(fe, 0.0) - jnp.minimum(fw, 0.0)) + (
                jnp.maximum(gn, 0.0) - jnp.minimum(gs, 0.0)
            )
            own = 1.0 - scale * out
            from_e, from_w = -scale * jnp.minimum(fe, 0.0), scale * jnp.maximum(fw, 0.0)
            from_n, from_s = -scale * jnp.minimum(gn, 0.0), scale * jnp.maximum(gs, 0.0)
            for n in range(nt):
                c = trp[n, l, mid(r), :]
                adv[l, r, n] = (
                    (own * c + from_e * roll(c, -1))
                    + (from_w * roll(c, 1) + from_n * trp[n, l, north(r), :])
                    + from_s * trp[n, l, south(r), :]
                )

    def advect_and_send(r):
        advect(r)

        @pl.when(jnp.logical_and(r > 1, r <= BULK_FIRST + 1))
        def _():
            send_bulk(r - 1)

    loop(1, blocks - 1, advect_and_send)

    s_first.wait_recv()

    def pair_density(r):
        spb[blk(r), :] = sb[blk(r), :] + srecv[0, blk(r), :]

    loop(0, blocks, pair_density)

    for load in loads[5:]:
        load.wait()

    def spread(n):
        for m in range(nt):
            kb[n, m] = jnp.full((8, lanes), kin[n, m], f32)

    loop(0, nt, spread)

    for there, copy in halo_recvs:

        @pl.when(there)
        def _(copy=copy):
            copy.wait_recv()

    s_second.start()

    for f, ref in enumerate(padded):
        ref[pl.ds(PAD - 1, 1), :] = ns_recv[0, pl.ds(f, 1), :]
        ref[pl.ds(PAD + rows, 1), :] = ns_recv[1, pl.ds(f, 1), :]
    d_south, w_south = dpp[pl.ds(PAD - 1, 1), :], wp[pl.ds(PAD - 1, 1), :]
    d_row, w_row = dpp[pl.ds(PAD, 1), :], wp[pl.ds(PAD, 1), :]
    depth_s = (0.5 / levels) * (d_south + d_row) * (w_south * w_row)
    for l in range(2):
        gp[l, pl.ds(PAD - 1, 1), :] = vp[l, pl.ds(PAD - 1, 1), :] * depth_s
    north_face(blocks - 1)

    def rim(r):
        m = jnp.where(even, roll(ew_recv[1, blk(r), :], -1), roll(ew_recv[0, blk(r), :], 1))
        mb[blk(r), :] = m
        d, w = dpp[mid(r), :], wp[mid(r), :]
        scale = (advect_rate * levels) / d
        depth_f = (0.5 / levels) * (d + unpacked(m, f_d)) * (w * unpacked(m, f_w))
        total = zero
        parts = []
        for l in range(2):
            flow = jnp.where(at_west, unpacked(m, n_uv + l), up[l, mid(r), :])
            flux = jnp.where(at_edge, flow * depth_f, 0.0)
            fe = fb[l, blk(r), :]
            total = total + (
                (fe - roll(fe, 1))
                + (gp[l, mid(r), :] - gp[l, south(r), :])
                + jnp.where(at_east, flux, -flux)
            )
            z = scale * flux
            z_e = jnp.broadcast_to(z[:, lanes - 1 : lanes], (8, lanes))
            z_w = jnp.broadcast_to(z[:, 0:1], (8, lanes))
            parts.append(jnp.where(even, -z_e, z_w))
        db[blk(r), :] = total
        zz = jnp.where(lane < 2 * nt, parts[0], parts[1])
        xb[blk(r), :] = jnp.minimum(zz, 0.0) * q[blk(r), :] + jnp.maximum(zz, 0.0) * m

    loop(0, blocks, rim)
    xt[...] = jnp.transpose(xb[...])
    advect(0)
    d_first.start()

    @pl.when(up_there)
    def _():
        x_up.start()

    @pl.when(down_there)
    def _():
        x_down.start()

    loop(BULK_FIRST + 1, BULK_SECOND + 1, send_bulk)
    advect(blocks - 1)

    d_first.wait_recv()

    def pair_divergence(r):
        dpb[blk(r), :] = db[blk(r), :] + drecv[0, blk(r), :]

    loop(0, blocks, pair_divergence)
    s_second.wait_recv()

    over_first = (lax.rem(g, 2) == 1).astype(f32)
    over_second = (g >= 2).astype(f32)
    press = baroclinic_rate / levels

    def pressure(r):
        over = over_first * srecv[0, blk(r), :] + over_second * srecv[1, blk(r), :]
        dens = [
            haline_coef * trp[0, l, mid(r), :] - thermal_coef * trp[1, l, mid(r), :] for l in range(2)
        ]
        d = press * dpp[mid(r), :]
        pp[0, blk(r), :] = d * (over + 0.5 * dens[0])
        pp[1, blk(r), :] = d * (over + dens[0] + 0.5 * dens[1])

    loop(0, blocks, pressure)
    d_second.start()
    loop(BULK_SECOND + 1, BULK_THIRD + 1, send_bulk)

    @pl.when(up_there)
    def _():
        x_down.wait_recv()

    @pl.when(down_there)
    def _():
        x_up.wait_recv()

    yb[...] = jnp.transpose(xr[...])
    mix_up = jnp.where(up_there, mixing_rate, 0.0).astype(f32)
    mix_down = jnp.where(down_there, mixing_rate, 0.0).astype(f32)
    own_up = (1.0 - mixing_rate) - mix_up
    own_down = (1.0 - mixing_rate) - mix_down

    def blend_edges(r):
        x = xb[blk(r), :]
        is_top = lane < 2 * nt
        other = jnp.where(is_top, roll(x, -2 * nt), roll(x, 2 * nt))
        bx[blk(r), :] = (
            jnp.where(is_top, own_up, own_down) * x
            + mixing_rate * other
            + jnp.where(is_top, mix_up, mix_down) * yb[blk(r), :]
        )

    loop(0, blocks, blend_edges)

    d_second.wait_recv()

    def surface(r):
        ns = sfb[blk(r), :] - eta_rate * wp[mid(r), :] * (dpb[blk(r), :] + drecv[1, blk(r), :])
        out_s[blk(r), :] = ns
        nsp[blk(r), :] = ns
        p0, p1 = pp[0, blk(r), :], pp[1, blk(r), :]
        c2[blk(r), :] = jnp.where(
            lane == 0, ns, jnp.where(lane == 1, roll(p0, 1), jnp.where(lane == 2, roll(p1, 2), 0.0))
        )

    loop(0, blocks, surface)
    r2[...] = zero
    r2[pl.ds(0, 1), :] = nsp[pl.ds(0, 1), :]
    for l in range(2):
        r2[pl.ds(1 + l, 1), :] = pp[l, pl.ds(0, 1), :]
    c2t[...] = jnp.transpose(c2[...])

    loop(BULK_THIRD + 1, blocks - 1, send_bulk)
    loop(0, 2, lambda i: send_bulk(i * (blocks - 1)))

    @pl.when(gt > 0)
    def _():
        p2_west.start()

    @pl.when(gy > 0)
    def _():
        p2_south.start()

    is_top_level = (g == 0).astype(f32)

    def finish(r):
        @pl.when(up_there)
        def _():
            bulk_down(r).wait_recv()

        @pl.when(down_there)
        def _():
            bulk_up(r).wait_recv()

        w = wp[mid(r), :]
        edge = bx[blk(r), :]
        updated = [[], []]
        for n in range(nt):
            a0, a1 = adv[0, r, n], adv[1, r, n]
            e0 = jnp.where(at_edge, unpacked(edge, n), 0.0)
            e1 = jnp.where(at_edge, unpacked(edge, nt + n), 0.0)
            b0 = (own_up * a0 + mixing_rate * a1) + (mix_up * ga[r, n] + e0)
            b1 = (own_down * a1 + mixing_rate * a0) + (mix_down * gb[r, n] + e1)
            for l, b in enumerate((b0, b1)):
                c = trp[n, l, mid(r), :]
                updated[l].append(c + w * (b - c))
        warm = [w * jnp.exp(warming_rate * updated[l][1]) for l in range(2)]
        cell = (r * 8 + sub) * lanes + lane
        top = is_top_level * w
        hits = [jnp.where(cell == rc[i], top, 0.0) for i in range(rc.shape[0])]
        for n in range(nt):
            k = kb[n, 0]
            react = [k * updated[l][0] for l in range(2)]
            for m in range(1, nt):
                k = kb[n, m]
                react = [react[l] + k * updated[l][m] for l in range(2)]
            source = hits[0] * rl[0, n]
            for i in range(1, rc.shape[0]):
                source = source + hits[i] * rl[i, n]
            out_tr[n, 0, blk(r), :] = updated[0][n] + (warm[0] * react[0] + source)
            out_tr[n, 1, blk(r), :] = updated[1][n] + warm[1] * react[1]

    half = blocks // 2
    loop(1, half + 1, finish)

    @pl.when(gt < n_tx - 1)
    def _():
        p2_west.wait_recv()

    @pl.when(gy < n_ty - 1)
    def _():
        p2_south.wait_recv()

    t2[...] = jnp.transpose(e2[...])
    nsp[pl.ds(rows, 1), :] = n2[pl.ds(0, 1), :]
    for l in range(2):
        pp[l, pl.ds(rows, 1), :] = n2[pl.ds(1 + l, 1), :]
    friction = jnp.where(g == n_grp - 1, friction_rate, 0.0).astype(f32)

    def velocities(r):
        m = mb[blk(r), :]
        t = t2[blk(r), :]
        w = wp[mid(r), :]
        open_e = w * jnp.where(at_east, unpacked(m, f_w), roll(w, -1))
        open_n = w * wp[north(r), :]
        above = pl.ds(r * 8 + 1, 8)
        ns = nsp[blk(r), :]
        slope_e = jnp.where(at_east, roll(t, -1), roll(ns, -1)) - ns
        slope_n = nsp[above, :] - ns
        for l in range(2):
            p = pp[l, blk(r), :]
            push_e = jnp.where(at_east, roll(t, -2 - l), roll(p, -1)) - p
            push_n = pp[l, above, :] - p
            for ref, out, field, opened, slope, push in (
                (up, out_u, n_uv + l, open_e, slope_e, push_e),
                (vp, out_v, n_uv + 2 + l, open_n, slope_n, push_n),
            ):
                x = ref[l, mid(r), :]
                beside = unpacked(m, field)
                lap = (
                    (ref[l, north(r), :] + ref[l, south(r), :])
                    + (jnp.where(at_east, beside, roll(x, -1)) + jnp.where(at_west, beside, roll(x, 1)))
                    - 4.0 * x
                )
                new = x - gravity_rate * slope - push + viscous_rate * lap
                if l == 1:
                    new = new - friction * x
                out[l, blk(r), :] = opened * new

    loop(0, blocks, velocities)
    loop(half + 1, blocks - 1, finish)
    loop(0, 2, lambda i: finish(i * (blocks - 1)))

    for copy in (s_first, s_second, d_first, d_second):
        copy.wait_send()
    for there, copy in halo_sends + [
        (up_there, x_up),
        (down_there, x_down),
        (gt > 0, p2_west),
        (gy > 0, p2_south),
    ]:

        @pl.when(there)
        def _(copy=copy):
            copy.wait_send()

    def sent(r):
        @pl.when(up_there)
        def _():
            bulk_up(r).wait_send()

        @pl.when(down_there)
        def _():
            bulk_down(r).wait_send()

    loop(0, blocks, sent)


def put_kernel(*refs):
    sources, targets, sem = refs[:4], refs[4:8], refs[8]
    puts = [pltpu.make_async_copy(a, b, sem.at[i]) for i, (a, b) in enumerate(zip(sources, targets))]
    for put in puts:
        put.start()
    for put in puts:
        put.wait()


def shards(tracers, east_velocity, north_velocity, surface, depth, wet_mask, river_cells, river_loads, kinetics):
    nt, own, rows, lanes = tracers.shape
    levels = own * lax.axis_size("grp")
    blocks = rows // 8
    tall = rows + 2 * PAD
    tile = pltpu.VMEM((rows, lanes), f32)
    twice = pltpu.VMEM((2, rows, lanes), f32)
    edges = pltpu.VMEM((2, 40, lanes), f32)
    dma = pltpu.SemaphoreType.DMA
    scratch = [
        pltpu.VMEM((nt, 2, tall, lanes), f32),
        pltpu.VMEM((2, tall, lanes), f32),
        pltpu.VMEM((2, tall, lanes), f32),
        tile,
        pltpu.VMEM((tall, lanes), f32),
        pltpu.VMEM((rows, lanes), jnp.int32),
        pltpu.VMEM((tall, lanes), f32),
        pltpu.VMEM((nt, nt, 8, lanes), f32),
        twice,
        pltpu.VMEM((2, tall, lanes), f32),
        tile,
        tile,
        twice,
        tile,
        tile,
        twice,
        edges,
        edges,
        tile,
        twice,
        tile,
        tile,
        tile,
        tile,
        tile,
        tile,
        pltpu.VMEM((2, blocks, nt, 8, lanes), f32),
        pltpu.VMEM((blocks, nt, 8, lanes), f32),
        pltpu.VMEM((blocks, nt, 8, lanes), f32),
        pltpu.VMEM((rows + 8, lanes), f32),
        pltpu.VMEM((2, rows + 8, lanes), f32),
        tile,
        tile,
        tile,
        tile,
        pltpu.VMEM((8, lanes), f32),
        pltpu.VMEM((8, lanes), f32),
        pltpu.SMEM(river_cells.shape, jnp.int32),
        pltpu.SMEM(river_loads.shape, f32),
        pltpu.SMEM((nt, nt), f32),
        dma((9,)),
        dma((4,)),
        dma((4,)),
        dma((4,)),
        dma((4,)),
        dma((2,)),
        dma((2,)),
        dma((2,)),
        dma((2,)),
        dma((2, blocks)),
        dma((2, blocks)),
    ]
    anywhere = pl.BlockSpec(memory_space=pltpu.HBM)
    vmem = pl.BlockSpec(memory_space=pltpu.VMEM)
    outs = (
        jax.ShapeDtypeStruct(tracers.shape, f32),
        jax.ShapeDtypeStruct(east_velocity.shape, f32),
        jax.ShapeDtypeStruct(north_velocity.shape, f32),
        jax.ShapeDtypeStruct(surface.shape, f32),
    )
    fields = [
        pltpu.with_memory_space_constraint(x, pltpu.HBM)
        for x in (
            tracers, east_velocity, north_velocity, surface, depth, wet_mask,
            river_cells, river_loads, kinetics,
        )
    ]
    results = pl.pallas_call(
        functools.partial(step_kernel, levels),
        out_shape=outs,
        in_specs=[anywhere] * 9,
        out_specs=(vmem,) * 4,
        scratch_shapes=scratch,
        compiler_params=pltpu.CompilerParams(
            collective_id=0, has_side_effects=True, vmem_limit_bytes=32 * 1024 * 1024
        ),
        name="estuary_step",
    )(*fields)
    return pl.pallas_call(
        put_kernel,
        out_shape=outs,
        in_specs=[pl.BlockSpec(memory_space=pl.ANY)] * 4,
        out_specs=(pl.BlockSpec(memory_space=pl.ANY),) * 4,
        scratch_shapes=[dma((4,))],
        compiler_params=pltpu.CompilerParams(vmem_limit_bytes=1024 * 1024),
        name="put",
    )(*results)


def solution(mesh):
    return jax.shard_map(
        shards,
        mesh=mesh,
        in_specs=(
            P(None, "grp", "ty", "tx"),
            P("grp", "ty", "tx"),
            P("grp", "ty", "tx"),
            P("ty", "tx"),
            P("ty", "tx"),
            P("ty", "tx"),
            P(("ty", "tx")),
            P(("ty", "tx"), None),
            P(),
        ),
        out_specs=(
            P(None, "grp", "ty", "tx"),
            P("grp", "ty", "tx"),
            P("grp", "ty", "tx"),
            P("ty", "tx"),
        ),
        check_vma=False,
    )
```

time: 206 us -> 39.7 us (0.19); the launches traced: 202 us -> 39.6 us
  other arithmetic: 85 us -> 0 us
  starting transfers between devices: 41.3 us -> 0 us
  Pallas kernels: 0 us -> 39 us
  local copies, waits for them, and re-layouts: 38.4 us -> 0 us
  waiting for transfers between devices: 20.1 us -> 0 us
  blocking collectives: 11.3 us -> 0 us
  matrix products: 4.7 us -> 0 us
    pallas_call x0 -> x2, Pallas kernels: none -> 39 us  [the longest x1 37.5 us: shards(): pl.pallas_call(functools.partial(step_kernel, levels), out_shape=outs, in...]
    ppermute x12 -> x0, starting transfers between devices: 36.9 us -> none  [the longest x5 21.4 us: extended(): lax.ppermute(tail, axis, [(i, (i + 1) % count) for i in range(ends)])]
    another operation x1 -> x0, other arithmetic: 28.5 us -> none  [shards(): running = jnp.cumsum(density, 0)]
    add x4 -> x0, other arithmetic: 24.8 us -> none  [the longest x1 11.6 us: advect(): jnp.maximum(east_speed, 0.0) * tracer_pad[..., 1:-1, :-1]]
    ppermute x12 -> x0, waiting for transfers between devices: 20.1 us -> none  [the longest x5 14.1 us: extended(): lax.ppermute(head, axis, [((i + 1) % count, i) for i in range(ends)])]
    slice x13 -> x0, local copies, waits for them, and re-layouts: 19.1 us -> none  [the longest x4 11.9 us: extended(): lax.slice_in_dim(cells, cells.shape[dim] - width, cells.shape[dim], axis=...]
    all_gather x1 -> x0, blocking collectives: 11.3 us -> none  [carried_in(): everything = lax.all_gather(value, axis)]
    unnamed x42 -> x0, local copies, waits for them, and re-layouts: 9.91 us -> none
  transfers between devices with their start and end apart: 13 -> 0, of which waited for: 6 -> 0; matrix products, arithmetic and copies ran while one was open for 43% -> 0% of each run, Pallas kernels for 0% -> 0%
where the time goes in v1:
time: 39.7 us; the launch traced here: 39.6 us
  Pallas kernels  39 us (98%)
  between operations  0.64 us (2%)
    pallas_call x1, Pallas kernels, shards(): pl.pallas_call(functools.partial(step_kernel, levels), out_shape=outs, in...  37.5 us
    pallas_call x1, Pallas kernels, shards(): pl.pallas_call(put_kernel, out_shape=outs, in_specs=[pl.BlockSpec(memory_...  1.44 us

profile of v1, /device:TPU:27, one launch (start us, length us, event | category | flops | bytes accessed | tf_op | source)
XLA Modules:
  0.0 39.6 jit_solution(12459476683252092050)
XLA Ops:
  0.6 37.5 %estuary_step.1 = (f32[16,2,128,128]{3,2,1,0:T(8,128)S(1)}, f32[2,128,128]{2,1,0:T(8,128)S(1)}, f32[2,128,128]{2,1,0:T(8,128)S(1)}, f32[128,128]{1,0:T(8,128)S(1)}) custom-call(f32[16,2,128,128]{3,2,1,0:T(8,128)} %tr_hbm.1, f32[2,128,128]{2,1,0:T(8,128)} %u_hbm.1, f32[2,128,128]{2,1,0:T(8,128)} %v_hbm.1, f32[128,128]{1,0:T(8,128)} %sf_hbm.1, ...), custom_call_target="tpu_custom_call" | custom-call | tf_op jit(solution)/shard_map/estuary_step/pallas_call | solution.py:651
  38.2 1.4 %put.1 = (f32[16,2,128,128]{3,2,1,0:T(8,128)}, f32[2,128,128]{2,1,0:T(8,128)}, f32[2,128,128]{2,1,0:T(8,128)}, f32[128,128]{1,0:T(8,128)}) custom-call(f32[16,2,128,128]{3,2,1,0:T(8,128)S(1)} %get-tuple-element.8.refs_0_, f32[2,128,128]{2,1,0:T(8,128)S(1)} %get-tuple-element.9.refs_1_, f32[2,128,128]{2,1,0:T(8,128)S(1)} %get-tuple-element.10.refs_2_, ...), custom_call_target="tpu_custom_call" | custom-call | tf_op jit(solution)/shard_map/put/pallas_call | solution.py:662

commit v2 on v1

v2 whole, which is shorter than its diff:
```python
import functools

import jax
import jax.numpy as jnp
from jax import lax
from jax.experimental import pallas as pl
from jax.experimental.pallas import tpu as pltpu
from jax.sharding import PartitionSpec as P

f32 = jnp.float32
MESH = pl.DeviceIdType.MESH

eta_rate = 0.25
gravity_rate = 0.25
baroclinic_rate = 0.4
viscous_rate = 0.1
friction_rate = 0.3
advect_rate = 0.3
mixing_rate = 0.2
haline_coef = 0.8
thermal_coef = 0.2
warming_rate = 0.46

PAD = 8
TALL = 32
BULK_FIRST = 2
VELOCITIES_AFTER = 5


def step_kernel(
    levels,
    tr_hbm, u_hbm, v_hbm, sf_hbm, dp_hbm, wm_hbm, rc_hbm, rl_hbm, kin_hbm,
    out_tr, out_u, out_v, out_s,
    trp, up, vp, sfb, dpp, wmb, wp, kb,
    fb, gp, sdb, sdp, sdr,
    ns_send, ns_recv, q, qt, ew_send, ew_recv, mt, mb,
    xb, xt, xr, er, yb, bx, adv, ga, gb,
    nsp, pp, c2, c2t, e2, t2, r2, n2,
    rc, rl, kin, load_sem, halo_ss, halo_rs, red_ss, red_rs, e_ss, e_rs, x_ss, x_rs, p2_ss, p2_rs, bulk_ss, bulk_rs,
):
    g, gy, gt = lax.axis_index("grp"), lax.axis_index("ty"), lax.axis_index("tx")
    n_grp, n_ty, n_tx = lax.axis_size("grp"), lax.axis_size("ty"), lax.axis_size("tx")
    nt = tr_hbm.shape[0]
    rows, lanes = sfb.shape
    blocks = rows // 8
    n_uv = 2 * nt
    f_d, f_w = n_uv + 4, n_uv + 5

    up_there, down_there = g > 0, g < n_grp - 1
    first = g + 1 - 2 * lax.rem(g, 2)
    second = n_grp - 1 - g
    third = lax.rem(g + n_grp // 2, n_grp)

    lane = lax.broadcasted_iota(jnp.int32, (8, lanes), 1)
    sub = lax.broadcasted_iota(jnp.int32, (8, lanes), 0)
    short_edge = jnp.logical_or(lane == lanes - 1, lane == 0)
    lane_t = lax.broadcasted_iota(jnp.int32, (TALL, lanes), 1)
    sub_t = lax.broadcasted_iota(jnp.int32, (TALL, lanes), 0)
    pair = lane_t // 2
    even = lax.rem(lane_t, 2) == 0
    at_east, at_west = lane_t == lanes - 1, lane_t == 0
    at_edge = jnp.logical_or(at_east, at_west)

    def roll(x, shift):
        shift = shift % lanes
        return x if shift == 0 else pltpu.roll(x, shift, 1)

    def unpacked(tile, field):
        return roll(tile, lanes - 1 - 2 * field)

    def blk(r):
        return pl.ds(pl.multiple_of(r * 8, 8), 8)

    def tall(i):
        return pl.ds(pl.multiple_of(i * TALL, TALL), TALL)

    def mid(r, n=8):
        return pl.ds(pl.multiple_of(r * n + PAD, 8), n)

    def south(r, n=8):
        return pl.ds(r * n + (PAD - 1), n)

    def north(r, n=8):
        return pl.ds(r * n + (PAD + 1), n)

    inner = pl.ds(PAD, rows)
    loads = [
        pltpu.make_async_copy(u_hbm, up.at[:, inner, :], load_sem.at[0]),
        pltpu.make_async_copy(v_hbm, vp.at[:, inner, :], load_sem.at[1]),
        pltpu.make_async_copy(dp_hbm, dpp.at[inner, :], load_sem.at[2]),
        pltpu.make_async_copy(wm_hbm, wmb, load_sem.at[3]),
        pltpu.make_async_copy(
            tr_hbm.at[pl.ds(0, 2)], trp.at[pl.ds(0, 2), :, inner, :], load_sem.at[4]
        ),
        pltpu.make_async_copy(
            tr_hbm.at[pl.ds(2, nt - 2)], trp.at[pl.ds(2, nt - 2), :, inner, :], load_sem.at[9]
        ),
        pltpu.make_async_copy(sf_hbm, sfb, load_sem.at[5]),
        pltpu.make_async_copy(kin_hbm, kin, load_sem.at[6]),
        pltpu.make_async_copy(rc_hbm, rc, load_sem.at[7]),
        pltpu.make_async_copy(rl_hbm, rl, load_sem.at[8]),
    ]
    for load in loads:
        load.start()

    neighbours = [
        (None, {"grp": first}),
        (None, {"grp": second}),
        (None, {"grp": third}),
        (gy > 0, {"ty": gy - 1}),
        (gy < n_ty - 1, {"ty": gy + 1}),
        (gt > 0, {"tx": gt - 1}),
        (gt < n_tx - 1, {"tx": gt + 1}),
    ]
    barrier = pltpu.get_barrier_semaphore()
    for there, device in neighbours:
        if there is None:
            pl.semaphore_signal(barrier, inc=1, device_id=device, device_id_type=MESH)
        else:

            @pl.when(there)
            def _(device=device):
                pl.semaphore_signal(barrier, inc=1, device_id=device, device_id_type=MESH)

    def remote(src, dst, ss, rs, device):
        return pltpu.make_async_remote_copy(
            src_ref=src, dst_ref=dst, send_sem=ss, recv_sem=rs, device_id=device, device_id_type=MESH
        )

    to_north = remote(ns_send.at[0], ns_recv.at[0], halo_ss.at[0], halo_rs.at[0], {"ty": gy + 1})
    to_south = remote(ns_send.at[1], ns_recv.at[1], halo_ss.at[1], halo_rs.at[1], {"ty": gy - 1})
    to_east = remote(ew_send.at[0], ew_recv.at[0], halo_ss.at[2], halo_rs.at[2], {"tx": gt + 1})
    to_west = remote(ew_send.at[1], ew_recv.at[1], halo_ss.at[3], halo_rs.at[3], {"tx": gt - 1})
    halo_sends = [
        (gy < n_ty - 1, to_north),
        (gy > 0, to_south),
        (gt < n_tx - 1, to_east),
        (gt > 0, to_west),
    ]
    halo_recvs = [
        (gy > 0, to_north),
        (gy < n_ty - 1, to_south),
        (gt > 0, to_east),
        (gt < n_tx - 1, to_west),
    ]
    sd_first = remote(sdb, sdr.at[0], red_ss.at[0], red_rs.at[0], {"grp": first})
    sd_second = remote(sdp, sdr.at[1], red_ss.at[1], red_rs.at[1], {"grp": second})
    flows = pl.ds(4 * nt, 8)
    flow_copies = [
        remote(xt.at[flows, :], er.at[i], e_ss.at[i], e_rs.at[i], {"grp": device})
        for i, device in enumerate((first, second, third))
    ]
    low, high = pl.ds(0, 2 * nt), pl.ds(2 * nt, 2 * nt)
    x_up = remote(xt.at[low, :], xr.at[high, :], x_ss.at[0], x_rs.at[0], {"grp": g - 1})
    x_down = remote(xt.at[high, :], xr.at[low, :], x_ss.at[1], x_rs.at[1], {"grp": g + 1})
    p2_west = remote(
        c2t.at[pl.ds(0, 8), :], e2.at[pl.ds(0, 8), :], p2_ss.at[0], p2_rs.at[0], {"tx": gt - 1}
    )
    p2_south = remote(r2, n2, p2_ss.at[1], p2_rs.at[1], {"ty": gy - 1})

    n_pairs = blocks // 2 - 1

    def blocks_of(i):
        return pl.ds(2 * i + 1, 2)

    def bulk_up(span, sem):
        return remote(adv.at[0, span], gb.at[span], bulk_ss.at[0, sem], bulk_rs.at[0, sem], {"grp": g - 1})

    def bulk_down(span, sem):
        return remote(adv.at[1, span], ga.at[span], bulk_ss.at[1, sem], bulk_rs.at[1, sem], {"grp": g + 1})

    def send_bulk(span, sem):
        @pl.when(up_there)
        def _():
            bulk_up(span, sem).start()

        @pl.when(down_there)
        def _():
            bulk_down(span, sem).start()

    def await_bulk(span, sem):
        @pl.when(up_there)
        def _():
            bulk_down(span, sem).wait_recv()

        @pl.when(down_there)
        def _():
            bulk_up(span, sem).wait_recv()

    def await_sent(span, sem):
        @pl.when(up_there)
        def _():
            bulk_up(span, sem).wait_send()

        @pl.when(down_there)
        def _():
            bulk_down(span, sem).wait_send()

    def single(i):
        return pl.ds(i * (blocks - 1), 1), n_pairs + i

    def couple(i):
        return blocks_of(i), i

    def loop(start, stop, body):
        lax.fori_loop(start, stop, lambda i, c: (body(i), c)[1], 0)

    zero = jnp.zeros((8, lanes), f32)
    zero_t = jnp.zeros((TALL, lanes), f32)
    talls = rows // TALL

    def clear(ref):
        def one(i):
            ref[blk(i), :] = zero

        loop(0, ref.shape[0] // 8, one)

    def clear_ghost(ref):
        def one(i):
            for n in range(nt):
                ref[i, n] = zero

        loop(0, blocks, one)

    @pl.when(jnp.logical_not(up_there))
    def _():
        clear_ghost(ga)
        clear(xr.at[low, :])

    @pl.when(jnp.logical_not(down_there))
    def _():
        clear_ghost(gb)
        clear(xr.at[high, :])

    clear(xr.at[pl.ds(4 * nt + 8, lanes - 4 * nt - 8), :])
    clear(mt.at[pl.ds(80, lanes - 80), :])
    clear(e2.at[pl.ds(8, lanes - 8), :])

    for slot, (there, _) in enumerate(halo_recvs):

        @pl.when(jnp.logical_not(there))
        def _(slot=slot):
            clear(ns_recv.at[slot] if slot < 2 else ew_recv.at[slot - 2])

    @pl.when(gt == n_tx - 1)
    def _():
        e2[pl.ds(0, 8), :] = zero

    @pl.when(gy == n_ty - 1)
    def _():
        n2[...] = zero

    for load in loads[:4]:
        load.wait()
    for edge in (0, PAD + rows):
        dpp[pl.ds(edge, 8), :] = zero
        wp[pl.ds(edge, 8), :] = zero
    for l in range(2):
        gp[l, pl.ds(0, 8), :] = zero

    def wetness(i):
        wp[mid(i, TALL), :] = wmb[tall(i), :].astype(f32)

    loop(0, talls, wetness)

    def north_face(i, n):
        d, w = dpp[mid(i, n), :], wp[mid(i, n), :]
        depth_n = (0.5 / levels) * (d + dpp[north(i, n), :]) * (w * wp[north(i, n), :])
        for l in range(2):
            gp[l, mid(i, n), :] = vp[l, mid(i, n), :] * depth_n

    def faces(i):
        d, w = dpp[mid(i, TALL), :], wp[mid(i, TALL), :]
        depth_e = (0.5 / levels) * (d + roll(d, -1)) * (w * roll(w, -1))
        depth_e = jnp.where(at_east, 0.0, depth_e)
        for l in range(2):
            fb[l, tall(i), :] = up[l, mid(i, TALL), :] * depth_e
        north_face(i, TALL)

    loop(0, talls, faces)

    def divergence(i):
        east = fb[0, tall(i), :] + fb[1, tall(i), :]
        in_n = gp[0, mid(i, TALL), :] + gp[1, mid(i, TALL), :]
        in_s = gp[0, south(i, TALL), :] + gp[1, south(i, TALL), :]
        sdb[1, tall(i), :] = (east - roll(east, 1)) + (in_n - in_s)

    loop(0, talls, divergence)
    loads[4].wait()

    def density(i):
        salt = trp[0, 0, mid(i, TALL), :] + trp[0, 1, mid(i, TALL), :]
        heat = trp[1, 0, mid(i, TALL), :] + trp[1, 1, mid(i, TALL), :]
        sdb[0, tall(i), :] = haline_coef * salt - thermal_coef * heat

    loop(0, talls, density)

    peers = sum(1 if there is None else there.astype(jnp.int32) for there, _ in neighbours)
    pl.semaphore_wait(barrier, peers)
    sd_first.start()

    loads[5].wait()

    def edges(i):
        packed = zero_t
        fields = [trp.at[n, l] for l in range(2) for n in range(nt)]
        fields += [up.at[0], up.at[1], vp.at[0], vp.at[1], dpp, wp]
        for f, field in enumerate(fields):
            packed = jnp.where(pair == f, roll(field[mid(i, TALL), :], 2 * f + 1), packed)
        q[tall(i), :] = packed

    loop(0, talls, edges)
    qt[...] = jnp.transpose(q[...])
    for side in range(2):
        ew_send[side] = qt[pl.ds(side, 40, stride=2), :]

    padded = [trp.at[n, l] for l in range(2) for n in range(nt)]
    padded += [up.at[0], up.at[1], vp.at[0], vp.at[1], dpp, wp]
    for slot in range(2):
        ns_send[slot, pl.ds(32, 8), :] = zero
    for f, ref in enumerate(padded):
        ns_send[0, pl.ds(f, 1), :] = ref[pl.ds(PAD + rows - 1, 1), :]
        ns_send[1, pl.ds(f, 1), :] = ref[pl.ds(PAD, 1), :]

    for there, copy in reversed(halo_sends):

        @pl.when(there)
        def _(copy=copy):
            copy.start()

    def advect(r):
        d = dpp[mid(r), :]
        scale = (advect_rate * levels) / d
        for l in range(2):
            fe, gn, gs = fb[l, blk(r), :], gp[l, mid(r), :], gp[l, south(r), :]
            fw = roll(fe, 1)
            out = (jnp.maximum(fe, 0.0) - jnp.minimum(fw, 0.0)) + (
                jnp.maximum(gn, 0.0) - jnp.minimum(gs, 0.0)
            )
            own = 1.0 - scale * out
            from_e, from_w = -scale * jnp.minimum(fe, 0.0), scale * jnp.maximum(fw, 0.0)
            from_n, from_s = -scale * jnp.minimum(gn, 0.0), scale * jnp.maximum(gs, 0.0)
            for n in range(nt):
                c = trp[n, l, mid(r), :]
                adv[l, r, n] = (
                    (own * c + from_e * roll(c, -1))
                    + (from_w * roll(c, 1) + from_n * trp[n, l, north(r), :])
                    + from_s * trp[n, l, south(r), :]
                )

    def advect_and_send(i):
        advect(2 * i + 1)
        advect(2 * i + 2)

        @pl.when(jnp.logical_and(i > 0, i <= BULK_FIRST))
        def _():
            send_bulk(*couple(i - 1))

    loop(0, n_pairs, advect_and_send)

    sd_first.wait_recv()

    def pair_sums(i):
        for k in range(2):
            sdp[k, tall(i), :] = sdb[k, tall(i), :] + sdr[0, k, tall(i), :]

    loop(0, talls, pair_sums)

    for load in loads[6:]:
        load.wait()

    def spread(n):
        for m in range(nt):
            kb[n, m] = jnp.full((8, lanes), kin[n, m], f32)

    loop(0, nt, spread)
    sd_second.start()

    for there, copy in halo_recvs:

        @pl.when(there)
        def _(copy=copy):
            copy.wait_recv()

    for f, ref in enumerate(padded):
        ref[pl.ds(PAD - 1, 1), :] = ns_recv[0, pl.ds(f, 1), :]
        ref[pl.ds(PAD + rows, 1), :] = ns_recv[1, pl.ds(f, 1), :]
    d_south, w_south = dpp[pl.ds(PAD - 1, 1), :], wp[pl.ds(PAD - 1, 1), :]
    d_row, w_row = dpp[pl.ds(PAD, 1), :], wp[pl.ds(PAD, 1), :]
    depth_s = (0.5 / levels) * (d_south + d_row) * (w_south * w_row)
    for l in range(2):
        gp[l, pl.ds(PAD - 1, 1), :] = vp[l, pl.ds(PAD - 1, 1), :] * depth_s
    north_face(blocks - 1, 8)
    for side in range(2):
        mt[pl.ds(side, 40, stride=2), :] = ew_recv[1 - side]
    mb[...] = jnp.transpose(mt[...])

    def rim(i):
        m = mb[tall(i), :]
        d, w = dpp[mid(i, TALL), :], wp[mid(i, TALL), :]
        scale = (advect_rate * levels) / d
        depth_f = (0.5 / levels) * (d + unpacked(m, f_d)) * (w * unpacked(m, f_w))
        total = zero_t
        parts = []
        for l in range(2):
            flow = jnp.where(at_west, unpacked(m, n_uv + l), up[l, mid(i, TALL), :])
            flux = jnp.where(at_edge, flow * depth_f, 0.0)
            total = total + jnp.where(at_east, flux, -flux)
            z = scale * flux
            z_e = jnp.broadcast_to(z[:, lanes - 1 : lanes], (TALL, lanes))
            z_w = jnp.broadcast_to(z[:, 0:1], (TALL, lanes))
            parts.append(jnp.where(even, -z_e, z_w))
        zz = jnp.where(lane_t < 2 * nt, parts[0], parts[1])
        x = jnp.minimum(zz, 0.0) * q[tall(i), :] + jnp.maximum(zz, 0.0) * m
        xb[tall(i), :] = jnp.where(pair == n_uv, roll(total, 2 * n_uv + 1), x)

    loop(0, talls, rim)
    xt[...] = jnp.transpose(xb[...])
    xt[pl.ds(4 * nt + 2, 1), :] = gp[0, pl.ds(PAD + rows - 1, 1), :] + gp[1, pl.ds(PAD + rows - 1, 1), :]
    xt[pl.ds(4 * nt + 3, 1), :] = -(gp[0, pl.ds(PAD - 1, 1), :] + gp[1, pl.ds(PAD - 1, 1), :])
    advect(0)
    for copy in reversed(flow_copies):
        copy.start()

    @pl.when(up_there)
    def _():
        x_up.start()

    @pl.when(down_there)
    def _():
        x_down.start()

    loop(BULK_FIRST, n_pairs, lambda i: send_bulk(*couple(i)))
    advect(blocks - 1)

    sd_second.wait_recv()
    over_first = (lax.rem(g, 2) == 1).astype(f32)
    over_second = (g >= 2).astype(f32)
    press = baroclinic_rate / levels

    def pressure(i):
        over = over_first * sdr[0, 0, tall(i), :] + over_second * sdr[1, 0, tall(i), :]
        dens = [
            haline_coef * trp[0, l, mid(i, TALL), :] - thermal_coef * trp[1, l, mid(i, TALL), :]
            for l in range(2)
        ]
        d = press * dpp[mid(i, TALL), :]
        pp[0, tall(i), :] = d * (over + 0.5 * dens[0])
        pp[1, tall(i), :] = d * (over + dens[0] + 0.5 * dens[1])

    loop(0, talls, pressure)
    loop(0, 2, lambda i: send_bulk(*single(i)))

    @pl.when(up_there)
    def _():
        x_down.wait_recv()

    @pl.when(down_there)
    def _():
        x_up.wait_recv()

    for copy in flow_copies:
        copy.wait_recv()
    flow_sum = (xt[flows, :] + er[0]) + (er[1] + er[2])
    xr[flows, :] = flow_sum
    yb[...] = jnp.transpose(xr[...])
    mix_up = jnp.where(up_there, mixing_rate, 0.0).astype(f32)
    mix_down = jnp.where(down_there, mixing_rate, 0.0).astype(f32)
    own_up = (1.0 - mixing_rate) - mix_up
    own_down = (1.0 - mixing_rate) - mix_down

    flow_n, flow_s = flow_sum[2:3, :], flow_sum[3:4, :]

    def surface(i):
        row = i * TALL + sub_t
        across = jnp.where(at_edge, unpacked(yb[tall(i), :], n_uv), 0.0)
        across = across + jnp.where(row == rows - 1, flow_n, jnp.where(row == 0, flow_s, 0.0))
        total = (sdp[1, tall(i), :] + sdr[1, 1, tall(i), :]) + across
        ns = sfb[tall(i), :] - eta_rate * wp[mid(i, TALL), :] * total
        out_s[tall(i), :] = ns
        nsp[tall(i), :] = ns
        p0, p1 = pp[0, tall(i), :], pp[1, tall(i), :]
        c2[tall(i), :] = jnp.where(
            lane_t == 0, ns, jnp.where(lane_t == 1, roll(p0, 1), jnp.where(lane_t == 2, roll(p1, 2), 0.0))
        )

    loop(0, talls, surface)
    r2[...] = zero
    r2[pl.ds(0, 1), :] = nsp[pl.ds(0, 1), :]
    for l in range(2):
        r2[pl.ds(1 + l, 1), :] = pp[l, pl.ds(0, 1), :]
    c2t[...] = jnp.transpose(c2[...])

    @pl.when(gt > 0)
    def _():
        p2_west.start()

    @pl.when(gy > 0)
    def _():
        p2_south.start()

    def blend_edges(i):
        x = xb[tall(i), :]
        is_top = lane_t < 2 * nt
        other = jnp.where(is_top, roll(x, -2 * nt), roll(x, 2 * nt))
        bx[tall(i), :] = (
            jnp.where(is_top, own_up, own_down) * x
            + mixing_rate * other
            + jnp.where(is_top, mix_up, mix_down) * yb[tall(i), :]
        )

    loop(0, talls, blend_edges)

    is_top_level = (g == 0).astype(f32)

    def finish(r):
        w = wp[mid(r), :]
        edge = bx[blk(r), :]
        updated = [[], []]
        for n in range(nt):
            a0, a1 = adv[0, r, n], adv[1, r, n]
            e0 = jnp.where(short_edge, unpacked(edge, n), 0.0)
            e1 = jnp.where(short_edge, unpacked(edge, nt + n), 0.0)
            b0 = (own_up * a0 + mixing_rate * a1) + (mix_up * ga[r, n] + e0)
            b1 = (own_down * a1 + mixing_rate * a0) + (mix_down * gb[r, n] + e1)
            for l, b in enumerate((b0, b1)):
                c = trp[n, l, mid(r), :]
                updated[l].append(c + w * (b - c))
        warm = [w * jnp.exp(warming_rate * updated[l][1]) for l in range(2)]
        cell = (r * 8 + sub) * lanes + lane
        top = is_top_level * w
        hits = [jnp.where(cell == rc[i], top, 0.0) for i in range(rc.shape[0])]
        for n in range(nt):
            k = kb[n, 0]
            react = [k * updated[l][0] for l in range(2)]
            for m in range(1, nt):
                k = kb[n, m]
                react = [react[l] + k * updated[l][m] for l in range(2)]
            source = hits[0] * rl[0, n]
            for i in range(1, rc.shape[0]):
                source = source + hits[i] * rl[i, n]
            out_tr[n, 0, blk(r), :] = updated[0][n] + (warm[0] * react[0] + source)
            out_tr[n, 1, blk(r), :] = updated[1][n] + warm[1] * react[1]

    def finish_couple(i):
        await_bulk(*couple(i))
        loop(2 * i + 1, 2 * i + 3, finish)

    def finish_single(i):
        await_bulk(*single(i))
        finish(i * (blocks - 1))

    loop(0, VELOCITIES_AFTER, finish_couple)

    @pl.when(gt < n_tx - 1)
    def _():
        p2_west.wait_recv()

    @pl.when(gy < n_ty - 1)
    def _():
        p2_south.wait_recv()

    t2[...] = jnp.transpose(e2[...])
    nsp[pl.ds(rows, 1), :] = n2[pl.ds(0, 1), :]
    for l in range(2):
        pp[l, pl.ds(rows, 1), :] = n2[pl.ds(1 + l, 1), :]
    friction = jnp.where(g == n_grp - 1, friction_rate, 0.0).astype(f32)

    def velocities(i):
        m = mb[tall(i), :]
        t = t2[tall(i), :]
        w = wp[mid(i, TALL), :]
        open_e = w * jnp.where(at_east, unpacked(m, f_w), roll(w, -1))
        open_n = w * wp[north(i, TALL), :]
        above = pl.ds(i * TALL + 1, TALL)
        ns = nsp[tall(i), :]
        slope_e = jnp.where(at_east, roll(t, -1), roll(ns, -1)) - ns
        slope_n = nsp[above, :] - ns
        for l in range(2):
            p = pp[l, tall(i), :]
            push_e = jnp.where(at_east, roll(t, -2 - l), roll(p, -1)) - p
            push_n = pp[l, above, :] - p
            for ref, out, field, opened, slope, push in (
                (up, out_u, n_uv + l, open_e, slope_e, push_e),
                (vp, out_v, n_uv + 2 + l, open_n, slope_n, push_n),
            ):
                x = ref[l, mid(i, TALL), :]
                beside = unpacked(m, field)
                lap = (
                    (ref[l, north(i, TALL), :] + ref[l, south(i, TALL), :])
                    + (jnp.where(at_east, beside, roll(x, -1)) + jnp.where(at_west, beside, roll(x, 1)))
                    - 4.0 * x
                )
                new = x - gravity_rate * slope - push + viscous_rate * lap
                if l == 1:
                    new = new - friction * x
                out[l, tall(i), :] = opened * new

    loop(0, talls, velocities)
    loop(VELOCITIES_AFTER, n_pairs, finish_couple)
    loop(0, 2, finish_single)

    for copy in [sd_first, sd_second, *flow_copies]:
        copy.wait_send()
    for there, copy in halo_sends + [
        (up_there, x_up),
        (down_there, x_down),
        (gt > 0, p2_west),
        (gy > 0, p2_south),
    ]:

        @pl.when(there)
        def _(copy=copy):
            copy.wait_send()

    loop(0, n_pairs, lambda i: await_sent(*couple(i)))
    loop(0, 2, lambda i: await_sent(*single(i)))


def put_kernel(*refs):
    sources, targets, sem = refs[:4], refs[4:8], refs[8]
    puts = [pltpu.make_async_copy(a, b, sem.at[i]) for i, (a, b) in enumerate(zip(sources, targets))]
    for put in puts:
        put.start()
    for put in puts:
        put.wait()


def shards(tracers, east_velocity, north_velocity, surface, depth, wet_mask, river_cells, river_loads, kinetics):
    nt, own, rows, lanes = tracers.shape
    levels = own * lax.axis_size("grp")
    blocks = rows // 8
    tall = rows + 2 * PAD
    tile = pltpu.VMEM((rows, lanes), f32)
    twice = pltpu.VMEM((2, rows, lanes), f32)
    edges = pltpu.VMEM((2, 40, lanes), f32)
    dma = pltpu.SemaphoreType.DMA
    scratch = [
        pltpu.VMEM((nt, 2, tall, lanes), f32),
        pltpu.VMEM((2, tall, lanes), f32),
        pltpu.VMEM((2, tall, lanes), f32),
        tile,
        pltpu.VMEM((tall, lanes), f32),
        pltpu.VMEM((rows, lanes), jnp.int32),
        pltpu.VMEM((tall, lanes), f32),
        pltpu.VMEM((nt, nt, 8, lanes), f32),
        twice,
        pltpu.VMEM((2, tall, lanes), f32),
        twice,
        twice,
        pltpu.VMEM((2, 2, rows, lanes), f32),
        edges,
        edges,
        tile,
        tile,
        edges,
        edges,
        tile,
        tile,
        tile,
        tile,
        tile,
        pltpu.VMEM((3, 8, lanes), f32),
        tile,
        tile,
        pltpu.VMEM((2, blocks, nt, 8, lanes), f32),
        pltpu.VMEM((blocks, nt, 8, lanes), f32),
        pltpu.VMEM((blocks, nt, 8, lanes), f32),
        pltpu.VMEM((rows + 8, lanes), f32),
        pltpu.VMEM((2, rows + 8, lanes), f32),
        tile,
        tile,
        tile,
        tile,
        pltpu.VMEM((8, lanes), f32),
        pltpu.VMEM((8, lanes), f32),
        pltpu.SMEM(river_cells.shape, jnp.int32),
        pltpu.SMEM(river_loads.shape, f32),
        pltpu.SMEM((nt, nt), f32),
        dma((10,)),
        dma((4,)),
        dma((4,)),
        dma((2,)),
        dma((2,)),
        dma((3,)),
        dma((3,)),
        dma((2,)),
        dma((2,)),
        dma((2,)),
        dma((2,)),
        dma((2, blocks)),
        dma((2, blocks)),
    ]
    anywhere = pl.BlockSpec(memory_space=pltpu.HBM)
    vmem = pl.BlockSpec(memory_space=pltpu.VMEM)
    outs = (
        jax.ShapeDtypeStruct(tracers.shape, f32),
        jax.ShapeDtypeStruct(east_velocity.shape, f32),
        jax.ShapeDtypeStruct(north_velocity.shape, f32),
        jax.ShapeDtypeStruct(surface.shape, f32),
    )
    fields = [
        pltpu.with_memory_space_constraint(x, pltpu.HBM)
        for x in (
            tracers, east_velocity, north_velocity, surface, depth, wet_mask,
            river_cells, river_loads, kinetics,
        )
    ]
    results = pl.pallas_call(
        functools.partial(step_kernel, levels),
        out_shape=outs,
        in_specs=[anywhere] * 9,
        out_specs=(vmem,) * 4,
        scratch_shapes=scratch,
        compiler_params=pltpu.CompilerParams(
            collective_id=0, has_side_effects=True, vmem_limit_bytes=32 * 1024 * 1024
        ),
        name="estuary_step",
    )(*fields)
    return pl.pallas_call(
        put_kernel,
        out_shape=outs,
        in_specs=[pl.BlockSpec(memory_space=pl.ANY)] * 4,
        out_specs=(pl.BlockSpec(memory_space=pl.ANY),) * 4,
        scratch_shapes=[dma((4,))],
        compiler_params=pltpu.CompilerParams(vmem_limit_bytes=1024 * 1024),
        name="put",
    )(*results)


def solution(mesh):
    return jax.shard_map(
        shards,
        mesh=mesh,
        in_specs=(
            P(None, "grp", "ty", "tx"),
            P("grp", "ty", "tx"),
            P("grp", "ty", "tx"),
            P("ty", "tx"),
            P("ty", "tx"),
            P("ty", "tx"),
            P(("ty", "tx")),
            P(("ty", "tx"), None),
            P(),
        ),
        out_specs=(
            P(None, "grp", "ty", "tx"),
            P("grp", "ty", "tx"),
            P("grp", "ty", "tx"),
            P("ty", "tx"),
        ),
        check_vma=False,
    )
```

time: 39.7 us -> 36.1 us (0.909)
  Pallas kernels: 39 us -> 35.3 us
    pallas_call x1, Pallas kernels: 37.5 us -> 33.9 us  [shards(): pl.pallas_call(functools.partial(step_kernel, levels), out_shape=outs, in...]
where the time goes in v2:
time: 36.1 us; the launch traced here: 35.9 us
  Pallas kernels  35.3 us (98%)
  between operations  0.64 us (2%)
    pallas_call x1, Pallas kernels, shards(): pl.pallas_call(functools.partial(step_kernel, levels), out_shape=outs, in...  33.9 us
    pallas_call x1, Pallas kernels, shards(): pl.pallas_call(put_kernel, out_shape=outs, in_specs=[pl.BlockSpec(memory_...  1.44 us

profile of v2, /device:TPU:27, one launch (start us, length us, event | category | flops | bytes accessed | tf_op | source)
XLA Modules:
  0.0 35.9 jit_solution(3052253821579630297)
XLA Ops:
  0.6 33.9 %estuary_step.1 = (f32[16,2,128,128]{3,2,1,0:T(8,128)S(1)}, f32[2,128,128]{2,1,0:T(8,128)S(1)}, f32[2,128,128]{2,1,0:T(8,128)S(1)}, f32[128,128]{1,0:T(8,128)S(1)}) custom-call(f32[16,2,128,128]{3,2,1,0:T(8,128)} %tr_hbm.1, f32[2,128,128]{2,1,0:T(8,128)} %u_hbm.1, f32[2,128,128]{2,1,0:T(8,128)} %v_hbm.1, f32[128,128]{1,0:T(8,128)} %sf_hbm.1, ...), custom_call_target="tpu_custom_call" | custom-call | tf_op jit(solution)/shard_map/estuary_step/pallas_call | solution.py:709
  34.5 1.4 %put.1 = (f32[16,2,128,128]{3,2,1,0:T(8,128)}, f32[2,128,128]{2,1,0:T(8,128)}, f32[2,128,128]{2,1,0:T(8,128)}, f32[128,128]{1,0:T(8,128)}) custom-call(f32[16,2,128,128]{3,2,1,0:T(8,128)S(1)} %get-tuple-element.8.refs_0_, f32[2,128,128]{2,1,0:T(8,128)S(1)} %get-tuple-element.9.refs_1_, f32[2,128,128]{2,1,0:T(8,128)S(1)} %get-tuple-element.10.refs_2_, ...), custom_call_target="tpu_custom_call" | custom-call | tf_op jit(solution)/shard_map/put/pallas_call | solution.py:720

commit v3 on v2

--- a/solution.py
+++ b/solution.py
@@ -23,8 +23,9 @@
 
 PAD = 8
 TALL = 32
-BULK_FIRST = 2
-VELOCITIES_AFTER = 5
+BULK_FIRST = 3
+BULK_MIDDLE = 4
+VELOCITIES_AFTER = 7
 
 
 def step_kernel(
@@ -32,7 +33,7 @@
     tr_hbm, u_hbm, v_hbm, sf_hbm, dp_hbm, wm_hbm, rc_hbm, rl_hbm, kin_hbm,
     out_tr, out_u, out_v, out_s,
     trp, up, vp, sfb, dpp, wmb, wp, kb,
-    fb, gp, sdb, sdp, sdr,
+    fb, gp, sdb, d_in, s_in, d_half, s_half, s_other, d_all, s_over,
     ns_send, ns_recv, q, qt, ew_send, ew_recv, mt, mb,
     xb, xt, xr, er, yb, bx, adv, ga, gb,
     nsp, pp, c2, c2t, e2, t2, r2, n2,
@@ -71,6 +72,9 @@
     def blk(r):
         return pl.ds(pl.multiple_of(r * 8, 8), 8)
 
+    def part(which, i):
+        return pl.ds(pl.multiple_of(which * (rows // 2) + i * TALL, TALL), TALL)
+
     def tall(i):
         return pl.ds(pl.multiple_of(i * TALL, TALL), TALL)
 
@@ -82,6 +86,25 @@
 
     def north(r, n=8):
         return pl.ds(r * n + (PAD + 1), n)
+
+    neighbours = [
+        (gt > 0, {"tx": gt - 1}),
+        (gt < n_tx - 1, {"tx": gt + 1}),
+        (None, {"grp": first}),
+        (None, {"grp": second}),
+        (None, {"grp": third}),
+        (gy > 0, {"ty": gy - 1}),
+        (gy < n_ty - 1, {"ty": gy + 1}),
+    ]
+    barrier = pltpu.get_barrier_semaphore()
+    for there, device in neighbours:
+        if there is None:
+            pl.semaphore_signal(barrier, inc=1, device_id=device, device_id_type=MESH)
+        else:
+
+            @pl.when(there)
+            def _(device=device):
+                pl.semaphore_signal(barrier, inc=1, device_id=device, device_id_type=MESH)
 
     inner = pl.ds(PAD, rows)
     loads = [
@@ -103,25 +126,6 @@
     for load in loads:
         load.start()
 
-    neighbours = [
-        (None, {"grp": first}),
-        (None, {"grp": second}),
-        (None, {"grp": third}),
-        (gy > 0, {"ty": gy - 1}),
-        (gy < n_ty - 1, {"ty": gy + 1}),
-        (gt > 0, {"tx": gt - 1}),
-        (gt < n_tx - 1, {"tx": gt + 1}),
-    ]
-    barrier = pltpu.get_barrier_semaphore()
-    for there, device in neighbours:
-        if there is None:
-            pl.semaphore_signal(barrier, inc=1, device_id=device, device_id_type=MESH)
-        else:
-
-            @pl.when(there)
-            def _(device=device):
-                pl.semaphore_signal(barrier, inc=1, device_id=device, device_id_type=MESH)
-
     def remote(src, dst, ss, rs, device):
         return pltpu.make_async_remote_copy(
             src_ref=src, dst_ref=dst, send_sem=ss, recv_sem=rs, device_id=device, device_id_type=MESH
@@ -143,8 +147,30 @@
         (gt > 0, to_east),
         (gt < n_tx - 1, to_west),
     ]
-    sd_first = remote(sdb, sdr.at[0], red_ss.at[0], red_rs.at[0], {"grp": first})
-    sd_second = remote(sdp, sdr.at[1], red_ss.at[1], red_rs.at[1], {"grp": second})
+    half = rows // 2
+    d_half_at, s_half_at = lax.rem((g + 1) // 2, 2), g // 2
+
+    def half_at(i):
+        return pl.ds(pl.multiple_of(i * half, half), half)
+
+    d_mine, d_other = half_at(d_half_at), half_at(1 - d_half_at)
+    s_mine, s_theirs = half_at(s_half_at), half_at(1 - s_half_at)
+
+    def reduction(i, src, dst, device):
+        return remote(src, dst, red_ss.at[i], red_rs.at[i], {"grp": device})
+
+    d_copies = [
+        reduction(0, sdb.at[1, d_other, :], d_in.at[0], first),
+        reduction(1, d_half, d_in.at[1], second),
+        reduction(2, d_all.at[d_mine, :], d_all.at[d_mine, :], first),
+    ]
+    s_copies = [
+        reduction(3, sdb.at[0, s_theirs, :], s_in.at[0], second),
+        reduction(4, s_half, s_in.at[1], first),
+        reduction(5, s_other, s_over.at[s_mine, :], second),
+    ]
+    d_last = reduction(2, d_all.at[d_other, :], d_all.at[d_other, :], first)
+    s_last = reduction(5, s_other, s_over.at[s_theirs, :], second)
     flows = pl.ds(4 * nt, 8)
     flow_copies = [
         remote(xt.at[flows, :], er.at[i], e_ss.at[i], e_rs.at[i], {"grp": device})
@@ -294,39 +320,6 @@
         sdb[0, tall(i), :] = haline_coef * salt - thermal_coef * heat
 
     loop(0, talls, density)
-
-    peers = sum(1 if there is None else there.astype(jnp.int32) for there, _ in neighbours)
-    pl.semaphore_wait(barrier, peers)
-    sd_first.start()
-
-    loads[5].wait()
-
-    def edges(i):
-        packed = zero_t
-        fields = [trp.at[n, l] for l in range(2) for n in range(nt)]
-        fields += [up.at[0], up.at[1], vp.at[0], vp.at[1], dpp, wp]
-        for f, field in enumerate(fields):
-            packed = jnp.where(pair == f, roll(field[mid(i, TALL), :], 2 * f + 1), packed)
-        q[tall(i), :] = packed
-
-    loop(0, talls, edges)
-    qt[...] = jnp.transpose(q[...])
-    for side in range(2):
-        ew_send[side] = qt[pl.ds(side, 40, stride=2), :]
-
-    padded = [trp.at[n, l] for l in range(2) for n in range(nt)]
-    padded += [up.at[0], up.at[1], vp.at[0], vp.at[1], dpp, wp]
-    for slot in range(2):
-        ns_send[slot, pl.ds(32, 8), :] = zero
-    for f, ref in enumerate(padded):
-        ns_send[0, pl.ds(f, 1), :] = ref[pl.ds(PAD + rows - 1, 1), :]
-        ns_send[1, pl.ds(f, 1), :] = ref[pl.ds(PAD, 1), :]
-
-    for there, copy in reversed(halo_sends):
-
-        @pl.when(there)
-        def _(copy=copy):
-            copy.start()
 
     def advect(r):
         d = dpp[mid(r), :]
@@ -348,23 +341,69 @@
                     + from_s * trp[n, l, south(r), :]
                 )
 
-    def advect_and_send(i):
+    def advect_couple(i):
         advect(2 * i + 1)
         advect(2 * i + 2)
 
-        @pl.when(jnp.logical_and(i > 0, i <= BULK_FIRST))
+    loads[5].wait()
+    loop(0, 1, advect_couple)
+
+    peers = sum(1 if there is None else there.astype(jnp.int32) for there, _ in neighbours)
+    pl.semaphore_wait(barrier, peers)
+    d_copies[0].start()
+    s_copies[0].start()
+
+    send_bulk(*couple(0))
+
+
+    def edges(i):
+        packed = zero_t
+        fields = [trp.at[n, l] for l in range(2) for n in range(nt)]
+        fields += [up.at[0], up.at[1], vp.at[0], vp.at[1], dpp, wp]
+        for f, field in enumerate(fields):
+            packed = jnp.where(pair == f, roll(field[mid(i, TALL), :], 2 * f + 1), packed)
+        q[tall(i), :] = packed
+
+    loop(0, talls, edges)
+    qt[...] = jnp.transpose(q[...])
+    for side in range(2):
+        ew_send[side] = qt[pl.ds(side, 40, stride=2), :]
+
+    padded = [trp.at[n, l] for l in range(2) for n in range(nt)]
+    padded += [up.at[0], up.at[1], vp.at[0], vp.at[1], dpp, wp]
+    for slot in range(2):
+        ns_send[slot, pl.ds(32, 8), :] = zero
+    for f, ref in enumerate(padded):
+        ns_send[0, pl.ds(f, 1), :] = ref[pl.ds(PAD + rows - 1, 1), :]
+        ns_send[1, pl.ds(f, 1), :] = ref[pl.ds(PAD, 1), :]
+
+    for there, copy in reversed(halo_sends):
+
+        @pl.when(there)
+        def _(copy=copy):
+            copy.start()
+
+    def advect_and_send(i):
+        advect_couple(i)
+
+        @pl.when(jnp.logical_and(i > 1, i <= BULK_FIRST))
         def _():
             send_bulk(*couple(i - 1))
 
-    loop(0, n_pairs, advect_and_send)
-
-    sd_first.wait_recv()
-
-    def pair_sums(i):
-        for k in range(2):
-            sdp[k, tall(i), :] = sdb[k, tall(i), :] + sdr[0, k, tall(i), :]
-
-    loop(0, talls, pair_sums)
+    loop(1, n_pairs, advect_and_send)
+
+    d_copies[0].wait_recv()
+    s_copies[0].wait_recv()
+    own_to_first = (g < n_grp - 1).astype(f32)
+    second_to_first = (g > 0).astype(f32)
+
+    def first_sums(i):
+        d_half[tall(i), :] = sdb[1, part(d_half_at, i), :] + d_in[0, tall(i), :]
+        s_half[tall(i), :] = (
+            own_to_first * sdb[0, part(s_half_at, i), :] + second_to_first * s_in[0, tall(i), :]
+        )
+
+    loop(0, half // TALL, first_sums)
 
     for load in loads[6:]:
         load.wait()
@@ -374,7 +413,9 @@
             kb[n, m] = jnp.full((8, lanes), kin[n, m], f32)
 
     loop(0, nt, spread)
-    sd_second.start()
+    d_copies[1].start()
+    s_copies[1].start()
+    loop(BULK_FIRST, BULK_MIDDLE, lambda i: send_bulk(*couple(i)))
 
     for there, copy in halo_recvs:
 
@@ -418,9 +459,23 @@
     xt[...] = jnp.transpose(xb[...])
     xt[pl.ds(4 * nt + 2, 1), :] = gp[0, pl.ds(PAD + rows - 1, 1), :] + gp[1, pl.ds(PAD + rows - 1, 1), :]
     xt[pl.ds(4 * nt + 3, 1), :] = -(gp[0, pl.ds(PAD - 1, 1), :] + gp[1, pl.ds(PAD - 1, 1), :])
+    d_copies[1].wait_recv()
+    s_copies[1].wait_recv()
+    above_1, above_2 = (g > 0).astype(f32), (g > 1).astype(f32)
+    other_1, other_2 = (g < n_grp - 1).astype(f32), (g < 2).astype(f32)
+
+    def second_sums(i):
+        d_all[part(d_half_at, i), :] = d_half[tall(i), :] + d_in[1, tall(i), :]
+        got = s_in[1, tall(i), :]
+        s_over[part(s_half_at, i), :] = above_1 * got + above_2 * s_in[0, tall(i), :]
+        s_other[tall(i), :] = other_1 * got + other_2 * sdb[0, part(s_half_at, i), :]
+
+    loop(0, half // TALL, second_sums)
     advect(0)
     for copy in reversed(flow_copies):
         copy.start()
+    d_copies[2].start()
+    s_copies[2].start()
 
     @pl.when(up_there)
     def _():
@@ -430,16 +485,16 @@
     def _():
         x_down.start()
 
-    loop(BULK_FIRST, n_pairs, lambda i: send_bulk(*couple(i)))
+    loop(BULK_MIDDLE, n_pairs, lambda i: send_bulk(*couple(i)))
     advect(blocks - 1)
 
-    sd_second.wait_recv()
-    over_first = (lax.rem(g, 2) == 1).astype(f32)
-    over_second = (g >= 2).astype(f32)
+    loop(0, 2, lambda i: send_bulk(*single(i)))
+
+    s_last.wait_recv()
     press = baroclinic_rate / levels
 
     def pressure(i):
-        over = over_first * sdr[0, 0, tall(i), :] + over_second * sdr[1, 0, tall(i), :]
+        over = s_over[tall(i), :]
         dens = [
             haline_coef * trp[0, l, mid(i, TALL), :] - thermal_coef * trp[1, l, mid(i, TALL), :]
             for l in range(2)
@@ -449,7 +504,6 @@
         pp[1, tall(i), :] = d * (over + dens[0] + 0.5 * dens[1])
 
     loop(0, talls, pressure)
-    loop(0, 2, lambda i: send_bulk(*single(i)))
 
     @pl.when(up_there)
     def _():
@@ -469,13 +523,14 @@
     own_up = (1.0 - mixing_rate) - mix_up
     own_down = (1.0 - mixing_rate) - mix_down
 
+    d_last.wait_recv()
     flow_n, flow_s = flow_sum[2:3, :], flow_sum[3:4, :]
 
     def surface(i):
         row = i * TALL + sub_t
         across = jnp.where(at_edge, unpacked(yb[tall(i), :], n_uv), 0.0)
         across = across + jnp.where(row == rows - 1, flow_n, jnp.where(row == 0, flow_s, 0.0))
-        total = (sdp[1, tall(i), :] + sdr[1, 1, tall(i), :]) + across
+        total = d_all[tall(i), :] + across
         ns = sfb[tall(i), :] - eta_rate * wp[mid(i, TALL), :] * total
         out_s[tall(i), :] = ns
         nsp[tall(i), :] = ns
@@ -600,7 +655,7 @@
     loop(VELOCITIES_AFTER, n_pairs, finish_couple)
     loop(0, 2, finish_single)
 
-    for copy in [sd_first, sd_second, *flow_copies]:
+    for copy in [*d_copies, *s_copies, *flow_copies]:
         copy.wait_send()
     for there, copy in halo_sends + [
         (up_there, x_up),
@@ -647,8 +702,13 @@
         twice,
         pltpu.VMEM((2, tall, lanes), f32),
         twice,
-        twice,
-        pltpu.VMEM((2, 2, rows, lanes), f32),
+        pltpu.VMEM((2, rows // 2, lanes), f32),
+        pltpu.VMEM((2, rows // 2, lanes), f32),
+        pltpu.VMEM((rows // 2, lanes), f32),
+        pltpu.VMEM((rows // 2, lanes), f32),
+        pltpu.VMEM((rows // 2, lanes), f32),
+        tile,
+        tile,
         edges,
         edges,
         tile,
@@ -680,8 +740,8 @@
         dma((10,)),
         dma((4,)),
         dma((4,)),
-        dma((2,)),
-        dma((2,)),
+        dma((6,)),
+        dma((6,)),
         dma((3,)),
         dma((3,)),
         dma((2,)),

time: 36.1 us -> 34.6 us (0.958)
  Pallas kernels: 35.3 us -> 33.5 us
    pallas_call x1, Pallas kernels: 33.9 us -> 32.1 us  [shards(): pl.pallas_call(functools.partial(step_kernel, levels), out_shape=outs, in...]
where the time goes in v3:
time: 34.6 us; the launch traced here: 34.2 us
  Pallas kernels  33.5 us (97%)
  between operations  0.64 us (2%)
    pallas_call x1, Pallas kernels, shards(): pl.pallas_call(functools.partial(step_kernel, levels), out_shape=outs, in...  32.1 us
    pallas_call x1, Pallas kernels, shards(): pl.pallas_call(put_kernel, out_shape=outs, in_specs=[pl.BlockSpec(memory_...  1.44 us

profile of v3, /device:TPU:27, one launch (start us, length us, event | category | flops | bytes accessed | tf_op | source)
XLA Modules:
  0.0 34.2 jit_solution(5415145777544596263)
XLA Ops:
  0.6 32.1 %estuary_step.1 = (f32[16,2,128,128]{3,2,1,0:T(8,128)S(1)}, f32[2,128,128]{2,1,0:T(8,128)S(1)}, f32[2,128,128]{2,1,0:T(8,128)S(1)}, f32[128,128]{1,0:T(8,128)S(1)}) custom-call(f32[16,2,128,128]{3,2,1,0:T(8,128)} %tr_hbm.1, f32[2,128,128]{2,1,0:T(8,128)} %u_hbm.1, f32[2,128,128]{2,1,0:T(8,128)} %v_hbm.1, f32[128,128]{1,0:T(8,128)} %sf_hbm.1, ...), custom_call_target="tpu_custom_call" | custom-call | tf_op jit(solution)/shard_map/estuary_step/pallas_call | solution.py:769
  32.7 1.4 %put.1 = (f32[16,2,128,128]{3,2,1,0:T(8,128)}, f32[2,128,128]{2,1,0:T(8,128)}, f32[2,128,128]{2,1,0:T(8,128)}, f32[128,128]{1,0:T(8,128)}) custom-call(f32[16,2,128,128]{3,2,1,0:T(8,128)S(1)} %get-tuple-element.8.refs_0_, f32[2,128,128]{2,1,0:T(8,128)S(1)} %get-tuple-element.9.refs_1_, f32[2,128,128]{2,1,0:T(8,128)S(1)} %get-tuple-element.10.refs_2_, ...), custom_call_target="tpu_custom_call" | custom-call | tf_op jit(solution)/shard_map/put/pallas_call | solution.py:780

commit v4 on v3

--- a/solution.py
+++ b/solution.py
@@ -354,6 +354,7 @@
     s_copies[0].start()
 
     send_bulk(*couple(0))
+    loop(1, 2, advect_couple)
 
 
     def edges(i):
@@ -377,6 +378,7 @@
         ns_send[0, pl.ds(f, 1), :] = ref[pl.ds(PAD + rows - 1, 1), :]
         ns_send[1, pl.ds(f, 1), :] = ref[pl.ds(PAD, 1), :]
 
+    send_bulk(*couple(1))
     for there, copy in reversed(halo_sends):
 
         @pl.when(there)
@@ -386,11 +388,11 @@
     def advect_and_send(i):
         advect_couple(i)
 
-        @pl.when(jnp.logical_and(i > 1, i <= BULK_FIRST))
+        @pl.when(jnp.logical_and(i > 2, i <= BULK_FIRST))
         def _():
             send_bulk(*couple(i - 1))
 
-    loop(1, n_pairs, advect_and_send)
+    loop(2, n_pairs, advect_and_send)
 
     d_copies[0].wait_recv()
     s_copies[0].wait_recv()

time: 34.6 us -> 34.6 us (level)
  no operation moved by 1% of the time
where the time goes in v4:
time: 34.6 us; the launch traced here: 34.2 us
  Pallas kernels  33.5 us (97%)
  between operations  0.64 us (2%)
    pallas_call x1, Pallas kernels, shards(): pl.pallas_call(functools.partial(step_kernel, levels), out_shape=outs, in...  32.1 us
    pallas_call x1, Pallas kernels, shards(): pl.pallas_call(put_kernel, out_shape=outs, in_specs=[pl.BlockSpec(memory_...  1.44 us

profile of v4, /device:TPU:27, one launch (start us, length us, event | category | flops | bytes accessed | tf_op | source)
XLA Modules:
  0.0 34.2 jit_solution(18251913632144085661)
XLA Ops:
  0.6 32.1 %estuary_step.1 = (f32[16,2,128,128]{3,2,1,0:T(8,128)S(1)}, f32[2,128,128]{2,1,0:T(8,128)S(1)}, f32[2,128,128]{2,1,0:T(8,128)S(1)}, f32[128,128]{1,0:T(8,128)S(1)}) custom-call(f32[16,2,128,128]{3,2,1,0:T(8,128)} %tr_hbm.1, f32[2,128,128]{2,1,0:T(8,128)} %u_hbm.1, f32[2,128,128]{2,1,0:T(8,128)} %v_hbm.1, f32[128,128]{1,0:T(8,128)} %sf_hbm.1, ...), custom_call_target="tpu_custom_call" | custom-call | tf_op jit(solution)/shard_map/estuary_step/pallas_call | solution.py:771
  32.7 1.4 %put.1 = (f32[16,2,128,128]{3,2,1,0:T(8,128)}, f32[2,128,128]{2,1,0:T(8,128)}, f32[2,128,128]{2,1,0:T(8,128)}, f32[128,128]{1,0:T(8,128)}) custom-call(f32[16,2,128,128]{3,2,1,0:T(8,128)S(1)} %get-tuple-element.8.refs_0_, f32[2,128,128]{2,1,0:T(8,128)S(1)} %get-tuple-element.9.refs_1_, f32[2,128,128]{2,1,0:T(8,128)S(1)} %get-tuple-element.10.refs_2_, ...), custom_call_target="tpu_custom_call" | custom-call | tf_op jit(solution)/shard_map/put/pallas_call | solution.py:782
